TPU v7x, 32 devices: a whole 2x2x4 slice. The times are simulated.
32 devices in a mesh: groups: 2 (over y), seq: 8 (over z, x), tp: 2 (over core).
Axes of the slice: x: 2, y: 2, z: 4, core: 2. Of those that a mesh axis runs over, the one named last changes fastest.
Arguments:
- span_queries: bfloat16 [128, 64, 128], P(('groups', 'seq'), 'tp'), parts along dimension 0, may hold values from -180 to 180
- span_keys: bfloat16 [128, 4, 128], P(('groups', 'seq'), 'tp'), parts along dimension 0, may hold values from -9 to 9
- span_values: bfloat16 [128, 4, 128], P(('groups', 'seq'), 'tp'), parts along dimension 0, may hold values from -6.5 to 6.5
- prefix_keys: bfloat16 [1152, 4, 128], P(('groups', 'seq'), 'tp'), parts along dimension 0, may hold values from -9 to 9
- prefix_values: bfloat16 [1152, 4, 128], P(('groups', 'seq'), 'tp'), parts along dimension 0, may hold values from -6.5 to 6.5
- prefix_lengths: int32 [16], P('groups'), parts along dimension 0, may hold values from 1 to 72
- decode_queries: bfloat16 [32, 64, 128], P(('groups', 'seq'), 'tp'), parts along dimension 0, may hold values from -180 to 180
- decode_new_keys: bfloat16 [32, 4, 128], P(('groups', 'seq'), 'tp'), parts along dimension 0, may hold values from -6 to 6
- decode_new_values: bfloat16 [32, 4, 128], P(('groups', 'seq'), 'tp'), parts along dimension 0, may hold values from -6 to 6
- decode_key_cache: bfloat16 [64, 256, 4, 128], P(('groups', 'seq'), None, 'tp'), parts along dimension 0, may hold values from -6 to 6
- decode_value_cache: bfloat16 [64, 256, 4, 128], P(('groups', 'seq'), None, 'tp'), parts along dimension 0, may hold values from -6 to 6
- owner_map: int32 [32, 1], P('groups'), parts along dimension 0, may hold values from 0 to 7; in each aligned block of 16 rows (0 to 15, 16 to 31, ...) at most 4 rows name the same one
- decode_lengths: int32 [32], P('groups'), parts along dimension 0, may hold values from 1 to 256
Outputs:
- prefill_out: bfloat16 [128, 64, 128], P(('groups', 'seq'), 'tp'), parts along dimension 0
- decode_out: bfloat16 [64, 64, 128], P(('groups', 'seq'), 'tp'), parts along dimension 0
There are 2 independent parts, one for each index of `groups`. A program takes and returns all parts, laid end to end along the dimension named above; each array names one. Nothing has to cross between parts.
Inputs may be any that keep to these rules, and one draw needn't show every extreme that they name: `owner_map`: no shard owns more than 4 requests, and some shard owns exactly 4.
All inputs are finite; a program needn't handle non-finite values.
Results may differ from a plain program's by a relative error of at most 0.005.
Values may be sent and summed in bfloat16 or wider, within the bound.
No kernel may reach another device: no remote copies, remote signals or barrier semaphores. Data moves between devices by JAX's collectives and lax.ppermute only.
A program may use at most 64 MiB of HBM per device.

v0:
```python
import math

import jax
import jax.numpy as jnp
from jax import lax
from jax.experimental import pallas as pl
from jax.experimental.pallas import tpu as pltpu
from jax.sharding import PartitionSpec as P


LOWEST = -1e30
FAR_AWAY = 1 << 30
PIECES = 8


def lookup_small(table, wanted):
    columns = jnp.arange(table.shape[0], dtype=jnp.int32)
    return jnp.sum(jnp.where(wanted[:, None] == columns[None, :], table[None, :], 0), axis=1)


def block_split(length):
    blocks = 1
    while length // blocks > 512 or length % blocks != 0:
        blocks += 1
    return blocks


def online_step(carried, queries, key_rows, value_rows, allowed):
    running_max, normalizer, weighted = carried
    scale = queries.shape[-1] ** (-0.5)
    scores = (
        jnp.einsum("tkgd,nkd->tkgn", queries, key_rows, preferred_element_type=jnp.float32) * scale
    )
    visible = allowed[:, None, None, :]
    scores = jnp.where(visible, scores, LOWEST)
    new_max = jnp.maximum(running_max, jnp.max(scores, axis=-1))
    weights = jnp.where(visible, jnp.exp(scores - new_max[..., None]), 0.0)
    factor = jnp.exp(running_max - new_max)
    normalizer = normalizer * factor + jnp.sum(weights, axis=-1)
    weighted = weighted * factor[..., None] + jnp.einsum(
        "tkgn,nkd->tkgd",
        weights.astype(jnp.bfloat16),
        value_rows,
        preferred_element_type=jnp.float32,
    )
    return (new_max, normalizer, weighted)


def guarded_step(carried, queries, key_rows, value_rows, allowed):
    return lax.cond(
        jnp.any(allowed),
        lambda inner: online_step(inner, queries, key_rows, value_rows, allowed),
        lambda inner: inner,
        carried,
    )


def fold_rows(carried, queries, key_rows, value_rows, allowed):
    length = key_rows.shape[0]
    blocks = block_split(length)
    if blocks == 1:
        return guarded_step(carried, queries, key_rows, value_rows, allowed)
    width = length // blocks
    stacked = (
        key_rows.reshape((blocks, width) + key_rows.shape[1:]),
        value_rows.reshape((blocks, width) + value_rows.shape[1:]),
        allowed.reshape(allowed.shape[0], blocks, width).transpose(1, 0, 2),
    )

    def visit(inner_carry, parts):
        return (guarded_step(inner_carry, queries, parts[0], parts[1], parts[2]), None)

    carried, _ = lax.scan(visit, carried, stacked)
    return carried


def on_large(
    span_queries,
    span_keys,
    span_values,
    prefix_keys,
    prefix_values,
    prefix_lengths,
    decode_queries,
    decode_new_keys,
    decode_new_values,
    decode_key_cache,
    decode_value_cache,
    owner_map,
    decode_lengths,
):
    device = lax.axis_index("seq")
    tokens_here, heads_here, head_dim = span_queries.shape
    kv_here = span_keys.shape[1]
    group_size = heads_here // kv_here
    queries = span_queries.reshape(tokens_here, kv_here, group_size, head_dim)
    token_index = device * tokens_here + jnp.arange(tokens_here, dtype=jnp.int32)
    prefix_here = prefix_keys.shape[0]
    initial = (
        jnp.full((tokens_here, kv_here, group_size), LOWEST, jnp.float32),
        jnp.zeros((tokens_here, kv_here, group_size), jnp.float32),
        jnp.zeros((tokens_here, kv_here, group_size, head_dim), jnp.float32),
    )
    stride = prefix_here + tokens_here
    both_keys = jnp.concatenate([prefix_keys, span_keys], axis=0)
    both_values = jnp.concatenate([prefix_values, span_values], axis=0)
    carried = initial
    key_rows = lax.all_gather(both_keys, "seq", axis=0, tiled=True)
    value_rows = lax.all_gather(both_values, "seq", axis=0, tiled=True)
    length = key_rows.shape[0]
    shards = length // stride
    tail = key_rows.shape[1:]
    keys_split = key_rows.reshape((shards, stride) + tail)
    values_split = value_rows.reshape((shards, stride) + tail)
    prefix_k = keys_split[:, :prefix_here].reshape((shards * prefix_here,) + tail)
    prefix_v = values_split[:, :prefix_here].reshape((shards * prefix_here,) + tail)
    span_k = keys_split[:, prefix_here:].reshape((shards * tokens_here,) + tail)
    span_v = values_split[:, prefix_here:].reshape((shards * tokens_here,) + tail)
    prefix_position = jnp.arange(shards * prefix_here, dtype=jnp.int32)
    prefix_ok = prefix_position % prefix_here < lookup_small(
        prefix_lengths, prefix_position // prefix_here
    )
    carried = fold_rows(
        carried,
        queries,
        prefix_k,
        prefix_v,
        jnp.broadcast_to(prefix_ok[None, :], (tokens_here, prefix_k.shape[0])),
    )
    span_position = jnp.arange(shards * tokens_here, dtype=jnp.int32)
    carried = fold_rows(
        carried, queries, span_k, span_v, span_position[None, :] <= token_index[:, None]
    )
    _, normalizer, weighted = carried
    prefill_out = (
        (weighted / normalizer[..., None])
        .reshape(tokens_here, heads_here, head_dim)
        .astype(jnp.bfloat16)
    )
    owners = owner_map[:, 0]
    requests = owners.shape[0]
    order = jnp.arange(requests, dtype=jnp.int32)
    earlier = (owners[None, :] == owners[:, None]) & (order[None, :] < order[:, None])
    ranking = jnp.sum(earlier.astype(jnp.int32), axis=1)
    slots_here = decode_key_cache.shape[0]
    slot_ids = jnp.arange(slots_here, dtype=jnp.int32)
    query_rows = lax.all_gather(decode_queries, "seq", axis=0, tiled=True)
    new_keys = lax.all_gather(decode_new_keys, "seq", axis=0, tiled=True)
    new_values = lax.all_gather(decode_new_values, "seq", axis=0, tiled=True)
    chosen = (owners == device)[None, :] & (ranking[None, :] == slot_ids[:, None])
    selector = chosen.astype(jnp.bfloat16)
    picked_queries = jnp.einsum(
        "sn,nhd->shd", selector, query_rows, preferred_element_type=jnp.float32
    )
    picked_keys = jnp.einsum("sn,nkd->skd", selector, new_keys, preferred_element_type=jnp.float32)
    picked_values = jnp.einsum(
        "sn,nkd->skd", selector, new_values, preferred_element_type=jnp.float32
    )
    picked_lengths = jnp.sum(jnp.where(chosen, decode_lengths[None, :], 0), axis=1)
    context = decode_key_cache.shape[1]
    grouped = picked_queries.astype(jnp.bfloat16).reshape(slots_here, kv_here, group_size, head_dim)
    own_keys = picked_keys.astype(jnp.bfloat16)
    own_values = picked_values.astype(jnp.bfloat16)
    scale = head_dim ** (-0.5)
    scores = (
        jnp.einsum("skgd,sckd->skgc", grouped, decode_key_cache, preferred_element_type=jnp.float32)
        * scale
    )
    visible = (jnp.arange(context, dtype=jnp.int32)[None, :] < picked_lengths[:, None])[
        :, None, None, :
    ]
    scores = jnp.where(visible, scores, LOWEST)
    own_score = (
        jnp.einsum("skgd,skd->skg", grouped, own_keys, preferred_element_type=jnp.float32) * scale
    )
    top_score = jnp.maximum(jnp.max(scores, axis=-1), own_score)
    weights = jnp.where(visible, jnp.exp(scores - top_score[..., None]), 0.0)
    own_weight = jnp.exp(own_score - top_score)
    total_weight = jnp.sum(weights, axis=-1) + own_weight
    rounded_own = lax.optimization_barrier(own_weight.astype(jnp.bfloat16)).astype(jnp.float32)
    mixed = jnp.einsum(
        "skgc,sckd->skgd",
        weights.astype(jnp.bfloat16),
        decode_value_cache,
        preferred_element_type=jnp.float32,
    )
    mixed = mixed + rounded_own[..., None] * own_values.astype(jnp.float32)[:, :, None, :]
    count_here = jnp.sum((owners == device).astype(jnp.int32))
    used = (slot_ids < count_here)[:, None, None, None]
    decode_out = (
        jnp.where(used, mixed / total_weight[..., None], 0.0)
        .reshape(slots_here, heads_here, head_dim)
        .astype(jnp.bfloat16)
    )
    return (prefill_out, decode_out)


class Sizes:
    def __init__(self, group, span_queries, span_keys, prefix_keys, decode_queries, cache):
        self.n = group
        self.half = group // 2
        self.tokens, self.heads, self.dim = span_queries.shape
        self.kv = span_keys.shape[1]
        self.share = self.heads // self.kv
        self.rows = self.tokens * self.heads
        self.pre = prefix_keys.shape[0]
        self.pre_rows = self.pre * self.kv
        self.block = self.pre_rows + self.tokens * self.kv
        self.cols = self.half * self.block
        self.asks = decode_queries.shape[0]
        self.ask_at = 2 * self.block
        self.new_at = self.ask_at + self.asks * self.heads
        self.new_rows = 2 * self.asks * self.kv
        self.pack = self.new_at + self.new_rows
        self.slots, self.context = cache.shape[:2]
        self.cache_rows = self.context * self.kv
        self.stat_rows = PIECES * self.rows // self.dim
        self.sel_at = self.rows + self.stat_rows
        self.sel_new_at = self.sel_at + self.slots * self.heads
        self.back = self.sel_new_at + self.slots * self.new_rows
        self.factor = self.dim**-0.5 * math.log2(math.e)

    def fits(self):
        power = self.n & (self.n - 1) == 0 and self.kv & (self.kv - 1) == 0
        return (
            power
            and 4 <= self.n <= 8
            and self.dim == 128
            and self.rows % 128 == 0
            and self.share % 16 == 0
            and self.block % 16 == 0
            and self.cols % 128 == 0
            and self.cache_rows % 128 == 0
            and self.new_rows == 8
        )


def column_tokens(z, me, table):
    lengths = [table[3 * z.slots + (me ^ j)] for j in range(z.half)]
    column = lax.broadcasted_iota(jnp.int32, (8, z.cols), 1)
    block = jnp.zeros((8, z.cols), jnp.int32)
    for j in range(1, z.half):
        block = block + (column >= z.block * j).astype(jnp.int32)
    within = column - block * z.block
    live = jnp.full((8, z.cols), lengths[0], jnp.int32)
    first = jnp.full((8, z.cols), me * z.tokens, jnp.int32)
    for j in range(1, z.half):
        live = jnp.where(block == j, lengths[j], live)
        first = jnp.where(block == j, (me ^ j) * z.tokens, first)
    place = within >> (z.kv.bit_length() - 1)
    token = jnp.where(
        within < z.pre_rows,
        jnp.where(place < live, -1, FAR_AWAY),
        first + place - z.pre,
    )
    head = within & (z.kv - 1)
    return [jnp.where(head == h, token, FAR_AWAY) for h in range(z.kv)]


def partial_attention(z, me, whose, query, near, table, score_ref, weight_ref, top_ref, sum_ref):
    keys = jnp.concatenate([b[0 : z.block, :] for b in near], axis=0)
    score_ref[...] = lax.dot_general(
        query[...], keys, (((1,), (1,)), ((), ())), preferred_element_type=jnp.float32
    )
    tokens = column_tokens(z, me, table)
    for t in range(z.tokens):
        for h in range(z.kv):
            at = t * z.heads + h * z.share
            seen = tokens[h] <= whose * z.tokens + t
            scores = score_ref[at : at + z.share, :].reshape(z.share // 8, 8, z.cols)
            scores = jnp.where(seen[None], scores, LOWEST)
            top = jnp.max(scores, axis=-1, keepdims=True)
            weights = jnp.exp2((scores - top) * z.factor)
            top_ref[at : at + z.share, :] = top.reshape(z.share, 1)
            sum_ref[at : at + z.share, :] = jnp.sum(weights, axis=-1, keepdims=True).reshape(
                z.share, 1
            )
            weight_ref[at : at + z.share, :] = weights.reshape(z.share, z.cols).astype(jnp.bfloat16)
    values = jnp.concatenate([b[z.block : 2 * z.block, :] for b in near], axis=0)
    return jnp.dot(weight_ref[...], values, preferred_element_type=jnp.float32)


def plan_kernel(z):
    def body(owners, lengths, cached, table):
        me = lax.axis_index("seq")
        partner = me ^ z.half
        for i in range(2 * z.slots):
            table[i] = -1

        def visit(r, counts):
            mine = owners[r] == me
            theirs = owners[r] == partner

            @pl.when(mine)
            def _():
                table[counts[0]] = r
                table[2 * z.slots + counts[0]] = cached[r]

            @pl.when(theirs)
            def _():
                table[z.slots + counts[1]] = r

            return (counts[0] + mine.astype(jnp.int32), counts[1] + theirs.astype(jnp.int32))

        lax.fori_loop(0, z.n * z.asks, visit, (jnp.int32(0), jnp.int32(0)))
        for i in range(z.n):
            table[3 * z.slots + i] = lengths[i]

    return body


def pick_near(z, me, near, request):
    ask = jnp.zeros((z.heads, z.dim), jnp.bfloat16)
    new = jnp.zeros((z.new_rows, z.dim), jnp.bfloat16)
    for j in range(z.half):
        for a in range(z.asks):
            hit = request == (me ^ j) * z.asks + a
            at = z.ask_at + a * z.heads
            ask = jnp.where(hit, near[j][at : at + z.heads, :], ask)
            if a == 0:
                new = jnp.where(
                    (request >= 0) & (lax.div(request, z.asks) == (me ^ j)),
                    near[j][z.new_at : z.pack, :],
                    new,
                )
    return ask, new


def pieces_of(x):
    first = x.astype(jnp.bfloat16).astype(jnp.float32)
    second = (x - first).astype(jnp.bfloat16).astype(jnp.float32)
    third = (x - first - second).astype(jnp.bfloat16).astype(jnp.float32)
    return [first, second, third]


def pack_kernel(z):
    def body(*refs):
        out, new, sems = refs[-3:]
        copies, at = [], 0
        for i, ref in enumerate(refs[:7]):
            rows = ref.shape[0]
            into = out.at[pl.ds(at, rows), :] if i < 5 else new.at[i - 5]
            copies.append(pltpu.make_async_copy(ref, into, sems.at[i]))
            at += rows
        for copy in reversed(copies):
            copy.start()
        for copy in reversed(copies):
            copy.wait()
        both = [new[i].astype(jnp.float32) for i in range(2)]
        out[z.new_at : z.pack, :] = jnp.concatenate(both, axis=0).astype(jnp.bfloat16)

    return body


def far_kernel(z):
    def body(table, query, *refs):
        near, back, scratch = refs[: z.half], refs[z.half], refs[z.half + 1 :]
        score_ref, weight_ref, top_ref, sum_ref = scratch
        me = lax.axis_index("seq")
        for s in range(z.slots):
            ask, new = pick_near(z, me, near, table[z.slots + s])
            at = z.sel_at + s * z.heads
            back[at : at + z.heads, :] = ask
            at = z.sel_new_at + s * z.new_rows
            back[at : at + z.new_rows, :] = new
        mixed = partial_attention(
            z, me, me ^ z.half, query, near, table, score_ref, weight_ref, top_ref, sum_ref
        )
        total = sum_ref[...]
        back[0 : z.rows, :] = (mixed / total).astype(jnp.bfloat16)
        lane = lax.broadcasted_iota(jnp.int32, (z.rows, z.dim), 1)
        packed = jnp.zeros((z.rows, z.dim), jnp.float32)
        for i, piece in enumerate(pieces_of(top_ref[...]) + pieces_of(total)):
            packed = jnp.where(lane == i, piece, packed)
        turned = jnp.transpose(packed)
        for i in range(z.rows // z.dim):
            back[z.rows + PIECES * i : z.rows + PIECES * (i + 1), :] = turned[
                :PIECES, i * z.dim : (i + 1) * z.dim
            ].astype(jnp.bfloat16)

    return body


def own_kernel(z):
    def body(table, query, *refs):
        near, (mixed, top_ref, sum_ref, mine), (score_ref, weight_ref) = (
            refs[: z.half],
            refs[z.half : z.half + 4],
            refs[z.half + 4 :],
        )
        me = lax.axis_index("seq")
        for s in range(z.slots):
            ask, new = pick_near(z, me, near, table[s])
            mine[s * z.heads : (s + 1) * z.heads, :] = ask
            at = z.slots * z.heads + s * z.new_rows
            mine[at : at + z.new_rows, :] = new
        mixed[...] = partial_attention(
            z, me, me, query, near, table, score_ref, weight_ref, top_ref, sum_ref
        )

    return body


def last_kernel(z):
    def body(
        table, mixed, top_ref, sum_ref, mine, back, keys, values, *outs
    ):
        out_hbm, decoded_hbm, out, decoded, sems = outs
        me = lax.axis_index("seq")
        turned = jnp.concatenate(
            [
                back[z.rows + PIECES * i : z.rows + PIECES * (i + 1), :].astype(jnp.float32)
                for i in range(z.rows // z.dim)
            ],
            axis=1,
        )
        packed = jnp.transpose(
            jnp.concatenate([turned, jnp.zeros((z.dim - PIECES, z.rows), jnp.float32)], axis=0)
        )
        far_top = packed[:, 0:1] + packed[:, 1:2] + packed[:, 2:3]
        far_sum = packed[:, 3:4] + packed[:, 4:5] + packed[:, 5:6]
        top = jnp.maximum(top_ref[...], far_top)
        here = jnp.exp2((top_ref[...] - top) * z.factor)
        there = jnp.exp2((far_top - top) * z.factor) * far_sum
        joined = mixed[...] * here + back[0 : z.rows, :].astype(jnp.float32) * there
        out[...] = (joined / (sum_ref[...] * here + there)).astype(jnp.bfloat16)
        first_copy = pltpu.make_async_copy(out, out_hbm, sems.at[0])
        first_copy.start()

        column = lax.broadcasted_iota(jnp.int32, (z.heads, z.cache_rows), 1)
        row = lax.broadcasted_iota(jnp.int32, (z.heads, z.cache_rows), 0)
        shift = z.share.bit_length() - 1
        match = (column & (z.kv - 1)) == (row >> shift)
        place = column >> (z.kv.bit_length() - 1)
        head_of = lax.broadcasted_iota(jnp.int32, (z.heads, z.dim), 0) >> shift
        for s in range(z.slots):
            request = table[s]
            used = request >= 0
            safe = jnp.maximum(request, 0)
            source = lax.div(safe, z.asks)
            at = safe - source * z.asks
            from_far = (source ^ me) >= z.half
            ask = jnp.where(
                from_far,
                back[z.sel_at + s * z.heads : z.sel_at + (s + 1) * z.heads, :],
                mine[s * z.heads : (s + 1) * z.heads, :],
            )
            first = z.slots * z.heads
            new = jnp.where(
                from_far,
                back[z.sel_new_at + s * z.new_rows : z.sel_new_at + (s + 1) * z.new_rows, :],
                mine[first + s * z.new_rows : first + (s + 1) * z.new_rows, :],
            ).astype(jnp.float32)
            new_key = jnp.zeros((z.heads, z.dim), jnp.float32)
            new_value = jnp.zeros((z.heads, z.dim), jnp.float32)
            for a in range(z.asks):
                for h in range(z.kv):
                    here_now = (head_of == h) & (at == a)
                    i = a * z.kv + h
                    new_key = jnp.where(here_now, new[i : i + 1, :], new_key)
                    i = i + z.asks * z.kv
                    new_value = jnp.where(here_now, new[i : i + 1, :], new_value)
            scores = lax.dot_general(
                ask,
                keys[s * z.cache_rows : (s + 1) * z.cache_rows, :],
                (((1,), (1,)), ((), ())),
                preferred_element_type=jnp.float32,
            )
            own = jnp.sum(ask.astype(jnp.float32) * new_key, axis=-1, keepdims=True)
            scores = jnp.where(match & (place < table[2 * z.slots + s]), scores, LOWEST)
            peak = jnp.maximum(jnp.max(scores, axis=-1, keepdims=True), own)
            weights = jnp.exp2((scores - peak) * z.factor)
            own_weight = jnp.exp2((own - peak) * z.factor)
            total = jnp.sum(weights, axis=-1, keepdims=True) + own_weight
            result = jnp.dot(
                weights.astype(jnp.bfloat16),
                values[s * z.cache_rows : (s + 1) * z.cache_rows, :],
                preferred_element_type=jnp.float32,
            )
            result = result + own_weight.astype(jnp.bfloat16).astype(jnp.float32) * new_value
            decoded[s * z.heads : (s + 1) * z.heads, :] = jnp.where(
                used, result / total, 0.0
            ).astype(jnp.bfloat16)
        second_copy = pltpu.make_async_copy(decoded, decoded_hbm, sems.at[1])
        second_copy.start()
        first_copy.wait()
        second_copy.wait()

    return body


def swap(x, n, by):
    return lax.ppermute(x, "seq", [(i, i ^ by) for i in range(n)])


def on_small(
    z,
    span_queries,
    span_keys,
    span_values,
    prefix_keys,
    prefix_values,
    prefix_lengths,
    decode_queries,
    decode_new_keys,
    decode_new_values,
    decode_key_cache,
    decode_value_cache,
    owner_map,
    decode_lengths,
):
    def flat(x):
        return x.reshape(-1, z.dim)

    def local(x):
        return pltpu.with_memory_space_constraint(x, pltpu.VMEM)

    smem = pl.BlockSpec(memory_space=pltpu.SMEM)
    vmem = pl.BlockSpec(memory_space=pltpu.VMEM)
    hbm = pl.BlockSpec(memory_space=pl.ANY)

    def ints(x):
        return pltpu.with_memory_space_constraint(x, pltpu.SMEM)

    queries = flat(span_queries)
    far_queries = local(swap(queries, z.n, z.half))
    packed = pl.pallas_call(
        pack_kernel(z),
        out_shape=pltpu.VMEM((z.pack, z.dim), jnp.bfloat16),
        in_specs=[hbm] * 7,
        out_specs=vmem,
        scratch_shapes=[
            pltpu.VMEM((2, z.asks * z.kv, z.dim), jnp.bfloat16),
            pltpu.SemaphoreType.DMA((7,)),
        ],
        name="pack",
    )(
        flat(prefix_keys),
        flat(span_keys),
        flat(prefix_values),
        flat(span_values),
        flat(decode_queries),
        flat(decode_new_keys),
        flat(decode_new_values),
    )
    near = [local(packed)]
    for j in range(1, z.half):
        near.append(local(swap(packed, z.n, j)))
    table = pl.pallas_call(
        plan_kernel(z),
        out_shape=pltpu.SMEM((3 * z.slots + z.n,), jnp.int32),
        in_specs=[smem] * 3,
        out_specs=smem,
        name="plan",
    )(owner_map.reshape(-1), prefix_lengths, decode_lengths)
    table = ints(table)
    wide = [pltpu.VMEM((z.rows, z.cols), jnp.float32), pltpu.VMEM((z.rows, z.cols), jnp.bfloat16)]
    thin = pltpu.VMEM((z.rows, 1), jnp.float32)
    sent = pl.pallas_call(
        far_kernel(z),
        out_shape=pltpu.VMEM((z.back, z.dim), jnp.bfloat16),
        in_specs=[smem] + [vmem] * (1 + z.half),
        out_specs=vmem,
        scratch_shapes=wide + [thin, thin],
        name="far_part",
    )(table, far_queries, *near)
    back = local(swap(sent, z.n, z.half))
    held = pl.pallas_call(
        own_kernel(z),
        out_shape=[
            pltpu.VMEM((z.rows, z.dim), jnp.float32),
            thin,
            thin,
            pltpu.VMEM((z.slots * (z.heads + z.new_rows), z.dim), jnp.bfloat16),
        ],
        in_specs=[smem] + [vmem] * (1 + z.half),
        out_specs=[vmem] * 4,
        scratch_shapes=wide,
        name="own_part",
    )(table, local(queries), *near)
    out, decoded = pl.pallas_call(
        last_kernel(z),
        out_shape=[
            jax.ShapeDtypeStruct((z.rows, z.dim), jnp.bfloat16),
            jax.ShapeDtypeStruct((z.slots * z.heads, z.dim), jnp.bfloat16),
        ],
        in_specs=[smem] + [vmem] * 7,
        out_specs=[hbm, hbm],
        scratch_shapes=[
            pltpu.VMEM((z.rows, z.dim), jnp.bfloat16),
            pltpu.VMEM((z.slots * z.heads, z.dim), jnp.bfloat16),
            pltpu.SemaphoreType.DMA((2,)),
        ],
        name="last_part",
    )(
        table,
        *[local(x) for x in held],
        back,
        local(flat(decode_key_cache)),
        local(flat(decode_value_cache)),
    )
    return (
        out.reshape(z.tokens, z.heads, z.dim),
        decoded.reshape(z.slots, z.heads, z.dim),
    )


def solution(mesh):
    group = mesh.shape["seq"]

    def on_device(*args):
        z = Sizes(group, args[0], args[1], args[3], args[6], args[9])
        if z.fits():
            return on_small(z, *args)
        return on_large(*args)

    return jax.shard_map(
        on_device,
        mesh=mesh,
        in_specs=(
            P(("groups", "seq"), "tp", None),
            P(("groups", "seq"), "tp", None),
            P(("groups", "seq"), "tp", None),
            P(("groups", "seq"), "tp", None),
            P(("groups", "seq"), "tp", None),
            P("groups"),
            P(("groups", "seq"), "tp", None),
            P(("groups", "seq"), "tp", None),
            P(("groups", "seq"), "tp", None),
            P(("groups", "seq"), None, "tp", None),
            P(("groups", "seq"), None, "tp", None),
            P("groups", None),
            P("groups"),
        ),
        out_specs=(P(("groups", "seq"), "tp", None), P(("groups", "seq"), "tp", None)),
        check_vma=False,
    )
```

profile of v0, /device:TPU:0, one launch (start us, length us, event | category | flops | bytes accessed | tf_op | source)
XLA Modules:
  0.0 23.0 jit_solution(5131187695665742487)
XLA Ops:
  0.6 0.0 copy-start.2
  0.6 1.0 %pack.1.refs_0_ = bf16[392,128]{1,0:T(8,128)(2,1)S(1)} custom-call(bf16[144,128]{1,0:T(8,128)(2,1)} %bitcast.17, bf16[16,128]{1,0:T(8,128)(2,1)} %bitcast.20, bf16[144,128]{1,0:T(8,128)(2,1)} %bitcast.18, bf16[16,128]{1,0:T(8,128)(2,1)} %bitcast.21, bf16[64,128]{1,0:T(8,128)(2,1)} %bitcast.19, bf16[4,128]{1,0:T(4,128)(2,1)} %bitcast.22, bf16[4,128]{1,0:T(4,128)(2,1)} %bitcast.23), custom_call_target="tpu_custom_call" | custom-call | tf_op jit(solution)/shard_map/pack/pallas_call | solution.py:527
  1.6 4.0 %collective-permute-start.2 = (bf16[392,128]{1,0:T(8,128)(2,1)S(1)}, bf16[392,128]{1,0:T(8,128)(2,1)S(1)}, u32[]{:S(2)}, u32[]{:S(2)}) collective-permute-start(bf16[392,128]{1,0:T(8,128)(2,1)S(1)} %pack.1.refs_0_), channel_id=1, source_target_pairs={{0,6},{2,4},{4,2},{6,0},{8,14},{10,12},{12,10},{14,8},{1,7},{3,5},... | collective-permute-start | bytes 301064 | tf_op jit(solution)/shard_map/ppermute | solution.py:493
  5.7 0.4 %collective-permute-start.1 = (bf16[392,128]{1,0:T(8,128)(2,1)S(1)}, bf16[392,128]{1,0:T(8,128)(2,1)S(1)}, u32[]{:S(2)}, u32[]{:S(2)}) collective-permute-start(bf16[392,128]{1,0:T(8,128)(2,1)S(1)} %pack.1.refs_0_), channel_id=1, source_target_pairs={{0,4},{2,6},{4,0},{6,2},{8,12},{10,14},{12,8},{14,10},{1,5},{3,7},... | collective-permute-start | bytes 301064 | tf_op jit(solution)/shard_map/ppermute | solution.py:493
  6.1 0.2 collective-permute-start
  6.3 0.0 copy-done.2
  6.3 2.9 %collective-permute-start.3 = (bf16[256,128]{1,0:T(8,128)(2,1)S(1)}, bf16[256,128]{1,0:T(8,128)(2,1)S(1)}, u32[]{:S(2)}, u32[]{:S(2)}) collective-permute-start(bf16[256,128]{1,0:T(8,128)(2,1)S(1)} %bitcast.15), channel_id=1, source_target_pairs={{0,8},{2,10},{4,12},{6,14},{8,0},{10,2},{12,4},{14,6},{1,9},{3,11}... | collective-permute-start | bytes 196616 | tf_op jit(solution)/shard_map/ppermute | solution.py:493
  9.2 0.9 %plan.1.table = s32[20]{0:T(128)S(4)} custom-call(s32[16]{0:T(128)} %bitcast.24, s32[8]{0:T(128)} %lengths.1, s32[16]{0:T(128)} %cached.1), custom_call_target="tpu_custom_call" | custom-call | tf_op jit(solution)/shard_map/plan/pallas_call | solution.py:549
  10.2 0.0 copy-start
  10.2 0.0 copy-start.1
  10.2 1.4 %collective-permute-done.3.query = bf16[256,128]{1,0:T(8,128)(2,1)S(1)} collective-permute-done((bf16[256,128]{1,0:T(8,128)(2,1)S(1)}, bf16[256,128]{1,0:T(8,128)(2,1)S(1)}, u32[]{:S(2)}, u32[]{:S(2)}) %collective-permute-start.3) | collective-permute-done | bytes 65568 | tf_op jit(solution)/shard_map/ppermute | solution.py:493
  11.6 0.0 collective-permute-done.2.refs_3_
  11.6 0.7 %collective-permute-done.1.refs_2_ = bf16[392,128]{1,0:T(8,128)(2,1)S(1)} collective-permute-done((bf16[392,128]{1,0:T(8,128)(2,1)S(1)}, bf16[392,128]{1,0:T(8,128)(2,1)S(1)}, u32[]{:S(2)}, u32[]{:S(2)}) %collective-permute-start.1) | collective-permute-done | bytes 100384 | tf_op jit(solution)/shard_map/ppermute | solution.py:493
  12.3 0.0 collective-permute-done.refs_1_
  12.3 0.9 %far_part.1 = bf16[432,128]{1,0:T(8,128)(2,1)S(1)} custom-call(s32[20]{0:T(128)S(4)} %plan.1.table, bf16[256,128]{1,0:T(8,128)(2,1)S(1)} %collective-permute-done.3.query, bf16[392,128]{1,0:T(8,128)(2,1)S(1)} %pack.1.refs_0_, bf16[392,128]{1,0:T(8,128)(2,1)S(1)} %collective-permute-done.refs_1_, bf16[392,128]{1,0:T(8,128)(2,1)S(1)} %collective-permute-done.1.refs_2_, ...), custom_call_target="tpu_custom_call" | custom-call | tf_op jit(solution)/shard_map/far_part/pallas_call | solution.py:559
  13.2 2.6 %collective-permute-start.4 = (bf16[432,128]{1,0:T(8,128)(2,1)S(1)}, bf16[432,128]{1,0:T(8,128)(2,1)S(1)}, u32[]{:S(2)}, u32[]{:S(2)}) collective-permute-start(bf16[432,128]{1,0:T(8,128)(2,1)S(1)} %far_part.1), channel_id=1, source_target_pairs={{0,8},{2,10},{4,12},{6,14},{8,0},{10,2},{12,4},{14,6},{1,9},{3,11}... | collective-permute-start | bytes 331784 | tf_op jit(solution)/shard_map/ppermute | solution.py:493
  15.7 0.6 %own_part.1 = (f32[256,128]{1,0:T(8,128)S(1)}, f32[256,1]{1,0:T(8,128)S(1)}, f32[256,1]{1,0:T(8,128)S(1)}, bf16[160,128]{1,0:T(8,128)(2,1)S(1)}) custom-call(s32[20]{0:T(128)S(4)} %plan.1.table, bf16[256,128]{1,0:T(8,128)(2,1)S(1)} %bitcast.16, bf16[392,128]{1,0:T(8,128)(2,1)S(1)} %pack.1.refs_0_, bf16[392,128]{1,0:T(8,128)(2,1)S(1)} %collective-permute-done.refs_1_, ...), custom_call_target="tpu_custom_call" | custom-call | tf_op jit(solution)/shard_map/own_part/pallas_call | solution.py:568
  16.4 4.8 %collective-permute-done.4.back = bf16[432,128]{1,0:T(8,128)(2,1)S(1)} collective-permute-done((bf16[432,128]{1,0:T(8,128)(2,1)S(1)}, bf16[432,128]{1,0:T(8,128)(2,1)S(1)}, u32[]{:S(2)}, u32[]{:S(2)}) %collective-permute-start.4) | collective-permute-done | bytes 110624 | tf_op jit(solution)/shard_map/ppermute | solution.py:493
  21.2 0.0 copy-done
  21.2 0.0 copy-done.1
  21.2 1.8 %last_part.1 = (bf16[256,128]{1,0:T(8,128)(2,1)}, bf16[128,128]{1,0:T(8,128)(2,1)}) custom-call(s32[20]{0:T(128)S(4)} %plan.1.table, f32[256,128]{1,0:T(8,128)S(1)} %get-tuple-element.8.mixed, f32[256,1]{1,0:T(8,128)S(1)} %get-tuple-element.9.top_ref, f32[256,1]{1,0:T(8,128)S(1)} %get-tuple-element.10.sum_ref, bf16[160,128]{1,0:T(8,128)(2,1)S(1)} %get-tuple-element.11.mine, ...), custom_call_target="tpu_custom_call" | custom-call | tf_op jit(solution)/shard_map/last_part/pallas_call | solution.py:581
Async XLA Ops:
  0.6 5.7 %copy-start.2 = (bf16[8,32,128]{2,1,0:T(8,128)(2,1)S(1)}, bf16[8,32,128]{2,1,0:T(8,128)(2,1)}, u32[]{:S(2)}) copy-start(bf16[8,32,128]{2,1,0:T(8,128)(2,1)} %param.13) | copy-start | bytes 196612
  1.6 10.0 %collective-permute-start.2 = (bf16[392,128]{1,0:T(8,128)(2,1)S(1)}, bf16[392,128]{1,0:T(8,128)(2,1)S(1)}, u32[]{:S(2)}, u32[]{:S(2)}) collective-permute-start(bf16[392,128]{1,0:T(8,128)(2,1)S(1)} %pack.1.refs_0_), channel_id=1, source_target_pairs={{0,6},{2,4},{4,2},{6,0},{8,14},{10,12},{12,10},{14,8},{1,7},{3,5},... | collective-permute-start | bytes 301064 | tf_op jit(solution)/shard_map/ppermute | solution.py:493
  5.7 6.6 %collective-permute-start.1 = (bf16[392,128]{1,0:T(8,128)(2,1)S(1)}, bf16[392,128]{1,0:T(8,128)(2,1)S(1)}, u32[]{:S(2)}, u32[]{:S(2)}) collective-permute-start(bf16[392,128]{1,0:T(8,128)(2,1)S(1)} %pack.1.refs_0_), channel_id=1, source_target_pairs={{0,4},{2,6},{4,0},{6,2},{8,12},{10,14},{12,8},{14,10},{1,5},{3,7},... | collective-permute-start | bytes 301064 | tf_op jit(solution)/shard_map/ppermute | solution.py:493
  6.1 6.2 %collective-permute-start = (bf16[392,128]{1,0:T(8,128)(2,1)S(1)}, bf16[392,128]{1,0:T(8,128)(2,1)S(1)}, u32[]{:S(2)}, u32[]{:S(2)}) collective-permute-start(bf16[392,128]{1,0:T(8,128)(2,1)S(1)} %pack.1.refs_0_), channel_id=1, source_target_pairs={{0,2},{2,0},{4,6},{6,4},{8,10},{10,8},{12,14},{14,12},{1,3},{3,1},... | collective-permute-start | bytes 301064 | tf_op jit(solution)/shard_map/ppermute | solution.py:493
  6.3 5.3 %collective-permute-start.3 = (bf16[256,128]{1,0:T(8,128)(2,1)S(1)}, bf16[256,128]{1,0:T(8,128)(2,1)S(1)}, u32[]{:S(2)}, u32[]{:S(2)}) collective-permute-start(bf16[256,128]{1,0:T(8,128)(2,1)S(1)} %bitcast.15), channel_id=1, source_target_pairs={{0,8},{2,10},{4,12},{6,14},{8,0},{10,2},{12,4},{14,6},{1,9},{3,11}... | collective-permute-start | bytes 196616 | tf_op jit(solution)/shard_map/ppermute | solution.py:493
  10.2 11.0 %copy-start = (bf16[4,256,2,128]{3,2,1,0:T(2,128)(2,1)S(1)}, bf16[4,256,2,128]{3,2,1,0:T(2,128)(2,1)}, u32[]{:S(2)}) copy-start(bf16[4,256,2,128]{3,2,1,0:T(2,128)(2,1)} %param.22) | copy-start | bytes 1572868
  10.2 11.0 %copy-start.1 = (bf16[4,256,2,128]{3,2,1,0:T(2,128)(2,1)S(1)}, bf16[4,256,2,128]{3,2,1,0:T(2,128)(2,1)}, u32[]{:S(2)}) copy-start(bf16[4,256,2,128]{3,2,1,0:T(2,128)(2,1)} %param.23) | copy-start | bytes 1572868
  13.2 8.0 %collective-permute-start.4 = (bf16[432,128]{1,0:T(8,128)(2,1)S(1)}, bf16[432,128]{1,0:T(8,128)(2,1)S(1)}, u32[]{:S(2)}, u32[]{:S(2)}) collective-permute-start(bf16[432,128]{1,0:T(8,128)(2,1)S(1)} %far_part.1), channel_id=1, source_target_pairs={{0,8},{2,10},{4,12},{6,14},{8,0},{10,2},{12,4},{14,6},{1,9},{3,11}... | collective-permute-start | bytes 331784 | tf_op jit(solution)/shard_map/ppermute | solution.py:493
where the time goes:
time: 23.2 us; the launch traced here: 23 us
  starting transfers between devices  10.2 us (44%)
  waiting for transfers between devices  6.91 us (30%)
  Pallas kernels  5.2 us (22%)
  between operations  0.69 us (3%)
    ppermute x5, starting transfers between devices, swap(): return lax.ppermute(x, 'seq', [(i, i ^ by) for i in range(n)])  10.2 us
    ppermute x5, waiting for transfers between devices, swap(): return lax.ppermute(x, 'seq', [(i, i ^ by) for i in range(n)])  6.91 us
    pallas_call x1, Pallas kernels, on_small(): pl.pallas_call(last_kernel(z), out_shape=[jax.ShapeDtypeStruct((z.rows, z...  1.8 us
    pallas_call x1, Pallas kernels, on_small(): pl.pallas_call(pack_kernel(z), out_shape=pltpu.VMEM((z.pack, z.dim), jnp....  0.96 us
    pallas_call x1, Pallas kernels, on_small(): pl.pallas_call(plan_kernel(z), out_shape=pltpu.SMEM((3 * z.slots + z.n,),...  0.93 us
    pallas_call x1, Pallas kernels, on_small(): pl.pallas_call(far_kernel(z), out_shape=pltpu.VMEM((z.back, z.dim), jnp.b...  0.89 us
    pallas_call x1, Pallas kernels, on_small(): pl.pallas_call(own_kernel(z), out_shape=[pltpu.VMEM((z.rows, z.dim), jnp....  0.62 us
  transfers between devices with their start and end apart: 5, of which 3 were waited for; matrix products, arithmetic and copies ran while one was open for 0% of the time, Pallas kernels for 7%

commit v1 on v0

--- a/solution.py
+++ b/solution.py
@@ -215,9 +215,10 @@
         self.slots, self.context = cache.shape[:2]
         self.cache_rows = self.context * self.kv
         self.stat_rows = PIECES * self.rows // self.dim
-        self.sel_at = self.rows + self.stat_rows
-        self.sel_new_at = self.sel_at + self.slots * self.heads
-        self.back = self.sel_new_at + self.slots * self.new_rows
+        self.pick_at = self.rows + self.stat_rows
+        self.pick_new_at = self.slots * self.heads
+        self.picks = self.pick_new_at + self.slots * self.new_rows
+        self.back = self.pick_at + self.picks
         self.factor = self.dim**-0.5 * math.log2(math.e)
 
     def fits(self):
@@ -271,10 +272,11 @@
             scores = jnp.where(seen[None], scores, LOWEST)
             top = jnp.max(scores, axis=-1, keepdims=True)
             weights = jnp.exp2((scores - top) * z.factor)
-            top_ref[at : at + z.share, :] = top.reshape(z.share, 1)
-            sum_ref[at : at + z.share, :] = jnp.sum(weights, axis=-1, keepdims=True).reshape(
-                z.share, 1
-            )
+            total = jnp.sum(weights, axis=-1, keepdims=True)
+            flat = (z.share, z.dim)
+            wide = (z.share // 8, 8, z.dim)
+            top_ref[at : at + z.share, :] = jnp.broadcast_to(top, wide).reshape(flat)
+            sum_ref[at : at + z.share, :] = jnp.broadcast_to(total, wide).reshape(flat)
             weight_ref[at : at + z.share, :] = weights.reshape(z.share, z.cols).astype(jnp.bfloat16)
     values = jnp.concatenate([b[z.block : 2 * z.block, :] for b in near], axis=0)
     return jnp.dot(weight_ref[...], values, preferred_element_type=jnp.float32)
@@ -352,30 +354,46 @@
     return body
 
 
+def turn_stats(z, top_ref, sum_ref):
+    lane = lax.broadcasted_iota(jnp.int32, (z.rows, z.dim), 1)
+    return jnp.transpose(jnp.where(lane == 0, top_ref[...], sum_ref[...]))[:8, :]
+
+
+def pick_all(z, me, table, first, near, out):
+    for s in range(z.slots):
+        ask, new = pick_near(z, me, near, table[first + s])
+        out[s * z.heads : (s + 1) * z.heads, :] = ask
+        at = z.pick_new_at + s * z.new_rows
+        out[at : at + z.new_rows, :] = new
+
+
+def select_kernel(z):
+    def body(table, *refs):
+        pick_all(z, lax.axis_index("seq"), table, z.slots, refs[:-1], refs[-1])
+
+    return body
+
+
 def far_kernel(z):
-    def body(table, query, *refs):
+    def body(table, query, asked, *refs):
         near, back, scratch = refs[: z.half], refs[z.half], refs[z.half + 1 :]
         score_ref, weight_ref, top_ref, sum_ref = scratch
         me = lax.axis_index("seq")
-        for s in range(z.slots):
-            ask, new = pick_near(z, me, near, table[z.slots + s])
-            at = z.sel_at + s * z.heads
-            back[at : at + z.heads, :] = ask
-            at = z.sel_new_at + s * z.new_rows
-            back[at : at + z.new_rows, :] = new
+        back[z.pick_at : z.back, :] = asked[...]
         mixed = partial_attention(
             z, me, me ^ z.half, query, near, table, score_ref, weight_ref, top_ref, sum_ref
         )
         total = sum_ref[...]
         back[0 : z.rows, :] = (mixed / total).astype(jnp.bfloat16)
-        lane = lax.broadcasted_iota(jnp.int32, (z.rows, z.dim), 1)
-        packed = jnp.zeros((z.rows, z.dim), jnp.float32)
-        for i, piece in enumerate(pieces_of(top_ref[...]) + pieces_of(total)):
-            packed = jnp.where(lane == i, piece, packed)
-        turned = jnp.transpose(packed)
+        stats = turn_stats(z, top_ref, sum_ref)
+        pieces = pieces_of(stats[0:1, :]) + pieces_of(stats[1:2, :])
+        row = lax.broadcasted_iota(jnp.int32, (PIECES, z.rows), 0)
+        turned = jnp.zeros((PIECES, z.rows), jnp.float32)
+        for i, piece in enumerate(pieces):
+            turned = jnp.where(row == i, piece, turned)
         for i in range(z.rows // z.dim):
             back[z.rows + PIECES * i : z.rows + PIECES * (i + 1), :] = turned[
-                :PIECES, i * z.dim : (i + 1) * z.dim
+                :, i * z.dim : (i + 1) * z.dim
             ].astype(jnp.bfloat16)
 
     return body
@@ -383,110 +401,114 @@
 
 def own_kernel(z):
     def body(table, query, *refs):
-        near, (mixed, top_ref, sum_ref, mine), (score_ref, weight_ref) = (
-            refs[: z.half],
-            refs[z.half : z.half + 4],
-            refs[z.half + 4 :],
-        )
+        near, (mixed, stats, mine) = refs[: z.half], refs[z.half : z.half + 3]
+        score_ref, weight_ref, top_ref, sum_ref = refs[z.half + 3 :]
         me = lax.axis_index("seq")
-        for s in range(z.slots):
-            ask, new = pick_near(z, me, near, table[s])
-            mine[s * z.heads : (s + 1) * z.heads, :] = ask
-            at = z.slots * z.heads + s * z.new_rows
-            mine[at : at + z.new_rows, :] = new
+        pick_all(z, me, table, 0, near, mine)
         mixed[...] = partial_attention(
             z, me, me, query, near, table, score_ref, weight_ref, top_ref, sum_ref
         )
+        stats[...] = turn_stats(z, top_ref, sum_ref)
 
     return body
 
 
 def last_kernel(z):
-    def body(
-        table, mixed, top_ref, sum_ref, mine, back, keys, values, *outs
-    ):
+    def body(table, mixed, stats, mine, back, keys, values, *outs):
         out_hbm, decoded_hbm, out, decoded, sems = outs
-        me = lax.axis_index("seq")
-        turned = jnp.concatenate(
+        pieces = jnp.concatenate(
             [
                 back[z.rows + PIECES * i : z.rows + PIECES * (i + 1), :].astype(jnp.float32)
                 for i in range(z.rows // z.dim)
             ],
             axis=1,
         )
-        packed = jnp.transpose(
-            jnp.concatenate([turned, jnp.zeros((z.dim - PIECES, z.rows), jnp.float32)], axis=0)
+        far_top = pieces[0:1, :] + pieces[1:2, :] + pieces[2:3, :]
+        far_sum = pieces[3:4, :] + pieces[4:5, :] + pieces[5:6, :]
+        own_top, own_sum = stats[0:1, :], stats[1:2, :]
+        top = jnp.maximum(own_top, far_top)
+        here = jnp.exp2((own_top - top) * z.factor)
+        there = jnp.exp2((far_top - top) * z.factor) * far_sum
+        inverse = 1.0 / (own_sum * here + there)
+        row = lax.broadcasted_iota(jnp.int32, (z.dim, z.rows), 0)
+        shares = jnp.transpose(jnp.where(row == 0, here * inverse, there * inverse))
+        joined = (
+            mixed[...] * shares[:, 0:1] + back[0 : z.rows, :].astype(jnp.float32) * shares[:, 1:2]
         )
-        far_top = packed[:, 0:1] + packed[:, 1:2] + packed[:, 2:3]
-        far_sum = packed[:, 3:4] + packed[:, 4:5] + packed[:, 5:6]
-        top = jnp.maximum(top_ref[...], far_top)
-        here = jnp.exp2((top_ref[...] - top) * z.factor)
-        there = jnp.exp2((far_top - top) * z.factor) * far_sum
-        joined = mixed[...] * here + back[0 : z.rows, :].astype(jnp.float32) * there
-        out[...] = (joined / (sum_ref[...] * here + there)).astype(jnp.bfloat16)
+        out[...] = joined.astype(jnp.bfloat16)
         first_copy = pltpu.make_async_copy(out, out_hbm, sems.at[0])
         first_copy.start()
-
-        column = lax.broadcasted_iota(jnp.int32, (z.heads, z.cache_rows), 1)
-        row = lax.broadcasted_iota(jnp.int32, (z.heads, z.cache_rows), 0)
-        shift = z.share.bit_length() - 1
-        match = (column & (z.kv - 1)) == (row >> shift)
-        place = column >> (z.kv.bit_length() - 1)
-        head_of = lax.broadcasted_iota(jnp.int32, (z.heads, z.dim), 0) >> shift
-        for s in range(z.slots):
-            request = table[s]
-            used = request >= 0
-            safe = jnp.maximum(request, 0)
-            source = lax.div(safe, z.asks)
-            at = safe - source * z.asks
-            from_far = (source ^ me) >= z.half
-            ask = jnp.where(
-                from_far,
-                back[z.sel_at + s * z.heads : z.sel_at + (s + 1) * z.heads, :],
-                mine[s * z.heads : (s + 1) * z.heads, :],
-            )
-            first = z.slots * z.heads
-            new = jnp.where(
-                from_far,
-                back[z.sel_new_at + s * z.new_rows : z.sel_new_at + (s + 1) * z.new_rows, :],
-                mine[first + s * z.new_rows : first + (s + 1) * z.new_rows, :],
-            ).astype(jnp.float32)
-            new_key = jnp.zeros((z.heads, z.dim), jnp.float32)
-            new_value = jnp.zeros((z.heads, z.dim), jnp.float32)
-            for a in range(z.asks):
-                for h in range(z.kv):
-                    here_now = (head_of == h) & (at == a)
-                    i = a * z.kv + h
-                    new_key = jnp.where(here_now, new[i : i + 1, :], new_key)
-                    i = i + z.asks * z.kv
-                    new_value = jnp.where(here_now, new[i : i + 1, :], new_value)
-            scores = lax.dot_general(
-                ask,
+        decode(z, table, mine, back, keys, values, decoded)
+        second_copy = pltpu.make_async_copy(decoded, decoded_hbm, sems.at[1])
+        second_copy.start()
+        first_copy.wait()
+        second_copy.wait()
+
+    return body
+
+
+def decode(z, table, mine, back, keys, values, decoded):
+    me = lax.axis_index("seq")
+    column = lax.broadcasted_iota(jnp.int32, (z.heads, z.cache_rows), 1)
+    row = lax.broadcasted_iota(jnp.int32, (z.heads, z.cache_rows), 0)
+    shift = z.share.bit_length() - 1
+    match = (column & (z.kv - 1)) == (row >> shift)
+    place = column >> (z.kv.bit_length() - 1)
+    head_of = lax.broadcasted_iota(jnp.int32, (z.heads, z.dim), 0) >> shift
+    asks, news, scores = [], [], []
+    for s in range(z.slots):
+        source = lax.div(jnp.maximum(table[s], 0), z.asks)
+        from_far = (source ^ me) >= z.half
+        here = s * z.heads
+        there = z.pick_at + here
+        ask = back[there : there + z.heads, :]
+        asks.append(jnp.where(from_far, ask, mine[here : here + z.heads, :]))
+        here = z.pick_new_at + s * z.new_rows
+        there = z.pick_at + here
+        new = back[there : there + z.new_rows, :]
+        new = jnp.where(from_far, new, mine[here : here + z.new_rows, :])
+        news.append(new.astype(jnp.float32))
+    for s in range(z.slots):
+        scores.append(
+            lax.dot_general(
+                asks[s],
                 keys[s * z.cache_rows : (s + 1) * z.cache_rows, :],
                 (((1,), (1,)), ((), ())),
                 preferred_element_type=jnp.float32,
             )
-            own = jnp.sum(ask.astype(jnp.float32) * new_key, axis=-1, keepdims=True)
-            scores = jnp.where(match & (place < table[2 * z.slots + s]), scores, LOWEST)
-            peak = jnp.maximum(jnp.max(scores, axis=-1, keepdims=True), own)
-            weights = jnp.exp2((scores - peak) * z.factor)
-            own_weight = jnp.exp2((own - peak) * z.factor)
-            total = jnp.sum(weights, axis=-1, keepdims=True) + own_weight
-            result = jnp.dot(
-                weights.astype(jnp.bfloat16),
-                values[s * z.cache_rows : (s + 1) * z.cache_rows, :],
-                preferred_element_type=jnp.float32,
-            )
-            result = result + own_weight.astype(jnp.bfloat16).astype(jnp.float32) * new_value
-            decoded[s * z.heads : (s + 1) * z.heads, :] = jnp.where(
-                used, result / total, 0.0
-            ).astype(jnp.bfloat16)
-        second_copy = pltpu.make_async_copy(decoded, decoded_hbm, sems.at[1])
-        second_copy.start()
-        first_copy.wait()
-        second_copy.wait()
-
-    return body
+        )
+    weights, rests = [], []
+    for s in range(z.slots):
+        safe = jnp.maximum(table[s], 0)
+        at = safe - lax.div(safe, z.asks) * z.asks
+        new = news[s]
+        new_key = jnp.zeros((z.heads, z.dim), jnp.float32)
+        new_value = jnp.zeros((z.heads, z.dim), jnp.float32)
+        for a in range(z.asks):
+            for h in range(z.kv):
+                here_now = (head_of == h) & (at == a)
+                i = a * z.kv + h
+                new_key = jnp.where(here_now, new[i : i + 1, :], new_key)
+                i = i + z.asks * z.kv
+                new_value = jnp.where(here_now, new[i : i + 1, :], new_value)
+        own = jnp.sum(asks[s].astype(jnp.float32) * new_key, axis=-1, keepdims=True)
+        seen = jnp.where(match & (place < table[2 * z.slots + s]), scores[s], LOWEST)
+        peak = jnp.maximum(jnp.max(seen, axis=-1, keepdims=True), own)
+        weight = jnp.exp2((seen - peak) * z.factor)
+        own_weight = jnp.exp2((own - peak) * z.factor)
+        total = jnp.sum(weight, axis=-1, keepdims=True) + own_weight
+        weights.append(weight.astype(jnp.bfloat16))
+        rests.append((own_weight.astype(jnp.bfloat16).astype(jnp.float32) * new_value, total))
+    for s in range(z.slots):
+        result = jnp.dot(
+            weights[s],
+            values[s * z.cache_rows : (s + 1) * z.cache_rows, :],
+            preferred_element_type=jnp.float32,
+        )
+        result = (result + rests[s][0]) / rests[s][1]
+        decoded[s * z.heads : (s + 1) * z.heads, :] = jnp.where(
+            table[s] >= 0, result, 0.0
+        ).astype(jnp.bfloat16)
 
 
 def swap(x, n, by):
@@ -554,27 +576,33 @@
         name="plan",
     )(owner_map.reshape(-1), prefix_lengths, decode_lengths)
     table = ints(table)
+    asked = pl.pallas_call(
+        select_kernel(z),
+        out_shape=pltpu.VMEM((z.picks, z.dim), jnp.bfloat16),
+        in_specs=[smem] + [vmem] * z.half,
+        out_specs=vmem,
+        name="select",
+    )(table, *near)
     wide = [pltpu.VMEM((z.rows, z.cols), jnp.float32), pltpu.VMEM((z.rows, z.cols), jnp.bfloat16)]
-    thin = pltpu.VMEM((z.rows, 1), jnp.float32)
+    wide += [pltpu.VMEM((z.rows, z.dim), jnp.float32)] * 2
     sent = pl.pallas_call(
         far_kernel(z),
         out_shape=pltpu.VMEM((z.back, z.dim), jnp.bfloat16),
-        in_specs=[smem] + [vmem] * (1 + z.half),
+        in_specs=[smem] + [vmem] * (2 + z.half),
         out_specs=vmem,
-        scratch_shapes=wide + [thin, thin],
+        scratch_shapes=wide,
         name="far_part",
-    )(table, far_queries, *near)
+    )(table, far_queries, local(asked), *near)
     back = local(swap(sent, z.n, z.half))
     held = pl.pallas_call(
         own_kernel(z),
         out_shape=[
             pltpu.VMEM((z.rows, z.dim), jnp.float32),
-            thin,
-            thin,
-            pltpu.VMEM((z.slots * (z.heads + z.new_rows), z.dim), jnp.bfloat16),
+            pltpu.VMEM((8, z.rows), jnp.float32),
+            pltpu.VMEM((z.picks, z.dim), jnp.bfloat16),
         ],
         in_specs=[smem] + [vmem] * (1 + z.half),
-        out_specs=[vmem] * 4,
+        out_specs=[vmem] * 3,
         scratch_shapes=wide,
         name="own_part",
     )(table, local(queries), *near)
@@ -584,7 +612,7 @@
             jax.ShapeDtypeStruct((z.rows, z.dim), jnp.bfloat16),
             jax.ShapeDtypeStruct((z.slots * z.heads, z.dim), jnp.bfloat16),
         ],
-        in_specs=[smem] + [vmem] * 7,
+        in_specs=[smem] + [vmem] * 6,
         out_specs=[hbm, hbm],
         scratch_shapes=[
             pltpu.VMEM((z.rows, z.dim), jnp.bfloat16),

time: 23.2 us -> 22.3 us (0.961)
  Pallas kernels: 5.2 us -> 4.37 us
    pallas_call x1, Pallas kernels: 1.8 us -> 1.21 us  [on_small(): pl.pallas_call(last_kernel(z), out_shape=[jax.ShapeDtypeStruct((z.rows, z...]
    pallas_call x1, Pallas kernels: 0.89 us -> 0.6 us  [on_small(): pl.pallas_call(far_kernel(z), out_shape=pltpu.VMEM((z.back, z.dim), jnp.b...]
  transfers between devices with their start and end apart: 5 -> 5, of which waited for: 3 -> 2; matrix products, arithmetic and copies ran while one was open for 0% -> 0% of each run, Pallas kernels for 7% -> 7%
where the time goes in v1:
time: 22.3 us; the launch traced here: 22.1 us
  starting transfers between devices  10.1 us (45%)
  waiting for transfers between devices  6.94 us (31%)
  Pallas kernels  4.37 us (20%)
  between operations  0.72 us (3%)
    ppermute x5, starting transfers between devices, swap(): return lax.ppermute(x, 'seq', [(i, i ^ by) for i in range(n)])  10.1 us
    ppermute x5, waiting for transfers between devices, swap(): return lax.ppermute(x, 'seq', [(i, i ^ by) for i in range(n)])  6.94 us
    pallas_call x1, Pallas kernels, on_small(): pl.pallas_call(last_kernel(z), out_shape=[jax.ShapeDtypeStruct((z.rows, z...  1.21 us
    pallas_call x1, Pallas kernels, on_small(): pl.pallas_call(pack_kernel(z), out_shape=pltpu.VMEM((z.pack, z.dim), jnp....  0.96 us
    pallas_call x1, Pallas kernels, on_small(): pl.pallas_call(plan_kernel(z), out_shape=pltpu.SMEM((3 * z.slots + z.n,),...  0.93 us
    pallas_call x1, Pallas kernels, on_small(): pl.pallas_call(own_kernel(z), out_shape=[pltpu.VMEM((z.rows, z.dim), jnp....  0.61 us
    pallas_call x1, Pallas kernels, on_small(): pl.pallas_call(far_kernel(z), out_shape=pltpu.VMEM((z.back, z.dim), jnp.b...  0.6 us
  transfers between devices with their start and end apart: 5, of which 2 were waited for; matrix products, arithmetic and copies ran while one was open for 0% of the time, Pallas kernels for 7%

profile of v1, /device:TPU:0, one launch (start us, length us, event | category | flops | bytes accessed | tf_op | source)
XLA Modules:
  0.0 22.1 jit_solution(7079757633356620304)
XLA Ops:
  0.6 0.0 copy-start.2
  0.6 1.0 %pack.1.refs_0_ = bf16[392,128]{1,0:T(8,128)(2,1)S(1)} custom-call(bf16[144,128]{1,0:T(8,128)(2,1)} %bitcast.17, bf16[16,128]{1,0:T(8,128)(2,1)} %bitcast.20, bf16[144,128]{1,0:T(8,128)(2,1)} %bitcast.18, bf16[16,128]{1,0:T(8,128)(2,1)} %bitcast.21, bf16[64,128]{1,0:T(8,128)(2,1)} %bitcast.19, bf16[4,128]{1,0:T(4,128)(2,1)} %bitcast.22, bf16[4,128]{1,0:T(4,128)(2,1)} %bitcast.23), custom_call_target="tpu_custom_call" | custom-call | tf_op jit(solution)/shard_map/pack/pallas_call | solution.py:549
  1.6 4.0 %collective-permute-start.2 = (bf16[392,128]{1,0:T(8,128)(2,1)S(1)}, bf16[392,128]{1,0:T(8,128)(2,1)S(1)}, u32[]{:S(2)}, u32[]{:S(2)}) collective-permute-start(bf16[392,128]{1,0:T(8,128)(2,1)S(1)} %pack.1.refs_0_), channel_id=1, source_target_pairs={{0,6},{2,4},{4,2},{6,0},{8,14},{10,12},{12,10},{14,8},{1,7},{3,5},... | collective-permute-start | bytes 301064 | tf_op jit(solution)/shard_map/ppermute | solution.py:515
  5.7 0.4 %collective-permute-start.1 = (bf16[392,128]{1,0:T(8,128)(2,1)S(1)}, bf16[392,128]{1,0:T(8,128)(2,1)S(1)}, u32[]{:S(2)}, u32[]{:S(2)}) collective-permute-start(bf16[392,128]{1,0:T(8,128)(2,1)S(1)} %pack.1.refs_0_), channel_id=1, source_target_pairs={{0,4},{2,6},{4,0},{6,2},{8,12},{10,14},{12,8},{14,10},{1,5},{3,7},... | collective-permute-start | bytes 301064 | tf_op jit(solution)/shard_map/ppermute | solution.py:515
  6.1 0.2 collective-permute-start
  6.3 0.0 copy-done.2
  6.3 2.9 %collective-permute-start.3 = (bf16[256,128]{1,0:T(8,128)(2,1)S(1)}, bf16[256,128]{1,0:T(8,128)(2,1)S(1)}, u32[]{:S(2)}, u32[]{:S(2)}) collective-permute-start(bf16[256,128]{1,0:T(8,128)(2,1)S(1)} %bitcast.15), channel_id=1, source_target_pairs={{0,8},{2,10},{4,12},{6,14},{8,0},{10,2},{12,4},{14,6},{1,9},{3,11}... | collective-permute-start | bytes 196616 | tf_op jit(solution)/shard_map/ppermute | solution.py:515
  9.2 0.9 %plan.1.table = s32[20]{0:T(128)S(4)} custom-call(s32[16]{0:T(128)} %bitcast.24, s32[8]{0:T(128)} %lengths.1, s32[16]{0:T(128)} %cached.1), custom_call_target="tpu_custom_call" | custom-call | tf_op jit(solution)/shard_map/plan/pallas_call | solution.py:571
  10.2 0.0 collective-permute-done.2.refs_3_
  10.2 2.1 %collective-permute-done.1.refs_2_ = bf16[392,128]{1,0:T(8,128)(2,1)S(1)} collective-permute-done((bf16[392,128]{1,0:T(8,128)(2,1)S(1)}, bf16[392,128]{1,0:T(8,128)(2,1)S(1)}, u32[]{:S(2)}, u32[]{:S(2)}) %collective-permute-start.1) | collective-permute-done | bytes 100384 | tf_op jit(solution)/shard_map/ppermute | solution.py:515
  12.3 0.0 collective-permute-done.refs_1_
  12.3 0.1 select.1.asked
  12.3 0.0 copy-start
  12.4 0.0 copy-start.1
  12.4 0.0 collective-permute-done.3.query
  12.4 0.6 %far_part.1 = bf16[432,128]{1,0:T(8,128)(2,1)S(1)} custom-call(s32[20]{0:T(128)S(4)} %plan.1.table, bf16[256,128]{1,0:T(8,128)(2,1)S(1)} %collective-permute-done.3.query, bf16[160,128]{1,0:T(8,128)(2,1)S(1)} %select.1.asked, bf16[392,128]{1,0:T(8,128)(2,1)S(1)} %pack.1.refs_0_, bf16[392,128]{1,0:T(8,128)(2,1)S(1)} %collective-permute-done.refs_1_, ...), custom_call_target="tpu_custom_call" | custom-call | tf_op jit(solution)/shard_map/far_part/pallas_call | solution.py:588
  13.0 2.5 %collective-permute-start.4 = (bf16[432,128]{1,0:T(8,128)(2,1)S(1)}, bf16[432,128]{1,0:T(8,128)(2,1)S(1)}, u32[]{:S(2)}, u32[]{:S(2)}) collective-permute-start(bf16[432,128]{1,0:T(8,128)(2,1)S(1)} %far_part.1), channel_id=1, source_target_pairs={{0,8},{2,10},{4,12},{6,14},{8,0},{10,2},{12,4},{14,6},{1,9},{3,11}... | collective-permute-start | bytes 331784 | tf_op jit(solution)/shard_map/ppermute | solution.py:515
  15.5 0.6 %own_part.1 = (f32[256,128]{1,0:T(8,128)S(1)}, f32[8,256]{1,0:T(8,128)S(1)}, bf16[160,128]{1,0:T(8,128)(2,1)S(1)}) custom-call(s32[20]{0:T(128)S(4)} %plan.1.table, bf16[256,128]{1,0:T(8,128)(2,1)S(1)} %bitcast.16, bf16[392,128]{1,0:T(8,128)(2,1)S(1)} %pack.1.refs_0_, bf16[392,128]{1,0:T(8,128)(2,1)S(1)} %collective-permute-done.refs_1_, ...), custom_call_target="tpu_custom_call" | custom-call | tf_op jit(solution)/shard_map/own_part/pallas_call | solution.py:597
  16.1 4.8 %collective-permute-done.4.back = bf16[432,128]{1,0:T(8,128)(2,1)S(1)} collective-permute-done((bf16[432,128]{1,0:T(8,128)(2,1)S(1)}, bf16[432,128]{1,0:T(8,128)(2,1)S(1)}, u32[]{:S(2)}, u32[]{:S(2)}) %collective-permute-start.4) | collective-permute-done | bytes 110624 | tf_op jit(solution)/shard_map/ppermute | solution.py:515
  20.9 0.0 copy-done
  20.9 0.0 copy-done.1
  20.9 1.2 %last_part.1 = (bf16[256,128]{1,0:T(8,128)(2,1)}, bf16[128,128]{1,0:T(8,128)(2,1)}) custom-call(s32[20]{0:T(128)S(4)} %plan.1.table, f32[256,128]{1,0:T(8,128)S(1)} %get-tuple-element.7.mixed, f32[8,256]{1,0:T(8,128)S(1)} %get-tuple-element.8.stats, bf16[160,128]{1,0:T(8,128)(2,1)S(1)} %get-tuple-element.9.mine, ...), custom_call_target="tpu_custom_call" | custom-call | tf_op jit(solution)/shard_map/last_part/pallas_call | solution.py:609
Async XLA Ops:
  0.6 5.7 %copy-start.2 = (bf16[8,32,128]{2,1,0:T(8,128)(2,1)S(1)}, bf16[8,32,128]{2,1,0:T(8,128)(2,1)}, u32[]{:S(2)}) copy-start(bf16[8,32,128]{2,1,0:T(8,128)(2,1)} %param.13) | copy-start | bytes 196612
  1.6 8.6 %collective-permute-start.2 = (bf16[392,128]{1,0:T(8,128)(2,1)S(1)}, bf16[392,128]{1,0:T(8,128)(2,1)S(1)}, u32[]{:S(2)}, u32[]{:S(2)}) collective-permute-start(bf16[392,128]{1,0:T(8,128)(2,1)S(1)} %pack.1.refs_0_), channel_id=1, source_target_pairs={{0,6},{2,4},{4,2},{6,0},{8,14},{10,12},{12,10},{14,8},{1,7},{3,5},... | collective-permute-start | bytes 301064 | tf_op jit(solution)/shard_map/ppermute | solution.py:515
  5.7 6.6 %collective-permute-start.1 = (bf16[392,128]{1,0:T(8,128)(2,1)S(1)}, bf16[392,128]{1,0:T(8,128)(2,1)S(1)}, u32[]{:S(2)}, u32[]{:S(2)}) collective-permute-start(bf16[392,128]{1,0:T(8,128)(2,1)S(1)} %pack.1.refs_0_), channel_id=1, source_target_pairs={{0,4},{2,6},{4,0},{6,2},{8,12},{10,14},{12,8},{14,10},{1,5},{3,7},... | collective-permute-start | bytes 301064 | tf_op jit(solution)/shard_map/ppermute | solution.py:515
  6.1 6.2 %collective-permute-start = (bf16[392,128]{1,0:T(8,128)(2,1)S(1)}, bf16[392,128]{1,0:T(8,128)(2,1)S(1)}, u32[]{:S(2)}, u32[]{:S(2)}) collective-permute-start(bf16[392,128]{1,0:T(8,128)(2,1)S(1)} %pack.1.refs_0_), channel_id=1, source_target_pairs={{0,2},{2,0},{4,6},{6,4},{8,10},{10,8},{12,14},{14,12},{1,3},{3,1},... | collective-permute-start | bytes 301064 | tf_op jit(solution)/shard_map/ppermute | solution.py:515
  6.3 6.1 %collective-permute-start.3 = (bf16[256,128]{1,0:T(8,128)(2,1)S(1)}, bf16[256,128]{1,0:T(8,128)(2,1)S(1)}, u32[]{:S(2)}, u32[]{:S(2)}) collective-permute-start(bf16[256,128]{1,0:T(8,128)(2,1)S(1)} %bitcast.15), channel_id=1, source_target_pairs={{0,8},{2,10},{4,12},{6,14},{8,0},{10,2},{12,4},{14,6},{1,9},{3,11}... | collective-permute-start | bytes 196616 | tf_op jit(solution)/shard_map/ppermute | solution.py:515
  12.3 8.6 %copy-start = (bf16[4,256,2,128]{3,2,1,0:T(2,128)(2,1)S(1)}, bf16[4,256,2,128]{3,2,1,0:T(2,128)(2,1)}, u32[]{:S(2)}) copy-start(bf16[4,256,2,128]{3,2,1,0:T(2,128)(2,1)} %param.22) | copy-start | bytes 1572868
  12.4 8.6 %copy-start.1 = (bf16[4,256,2,128]{3,2,1,0:T(2,128)(2,1)S(1)}, bf16[4,256,2,128]{3,2,1,0:T(2,128)(2,1)}, u32[]{:S(2)}) copy-start(bf16[4,256,2,128]{3,2,1,0:T(2,128)(2,1)} %param.23) | copy-start | bytes 1572868
  13.0 7.9 %collective-permute-start.4 = (bf16[432,128]{1,0:T(8,128)(2,1)S(1)}, bf16[432,128]{1,0:T(8,128)(2,1)S(1)}, u32[]{:S(2)}, u32[]{:S(2)}) collective-permute-start(bf16[432,128]{1,0:T(8,128)(2,1)S(1)} %far_part.1), channel_id=1, source_target_pairs={{0,8},{2,10},{4,12},{6,14},{8,0},{10,2},{12,4},{14,6},{1,9},{3,11}... | collective-permute-start | bytes 331784 | tf_op jit(solution)/shard_map/ppermute | solution.py:515

commit v2 on v1

--- a/solution.py
+++ b/solution.py
@@ -199,6 +199,8 @@
     def __init__(self, group, span_queries, span_keys, prefix_keys, decode_queries, cache):
         self.n = group
         self.half = group // 2
+        self.far = self.half
+        self.offsets = [j for j in range(group) if not j & self.far]
         self.tokens, self.heads, self.dim = span_queries.shape
         self.kv = span_keys.shape[1]
         self.share = self.heads // self.kv
@@ -237,7 +239,7 @@
 
 
 def column_tokens(z, me, table):
-    lengths = [table[3 * z.slots + (me ^ j)] for j in range(z.half)]
+    lengths = [table[3 * z.slots + (me ^ j)] for j in z.offsets]
     column = lax.broadcasted_iota(jnp.int32, (8, z.cols), 1)
     block = jnp.zeros((8, z.cols), jnp.int32)
     for j in range(1, z.half):
@@ -247,7 +249,7 @@
     first = jnp.full((8, z.cols), me * z.tokens, jnp.int32)
     for j in range(1, z.half):
         live = jnp.where(block == j, lengths[j], live)
-        first = jnp.where(block == j, (me ^ j) * z.tokens, first)
+        first = jnp.where(block == j, (me ^ z.offsets[j]) * z.tokens, first)
     place = within >> (z.kv.bit_length() - 1)
     token = jnp.where(
         within < z.pre_rows,
@@ -285,7 +287,7 @@
 def plan_kernel(z):
     def body(owners, lengths, cached, table):
         me = lax.axis_index("seq")
-        partner = me ^ z.half
+        partner = me ^ z.far
         for i in range(2 * z.slots):
             table[i] = -1
 
@@ -316,12 +318,12 @@
     new = jnp.zeros((z.new_rows, z.dim), jnp.bfloat16)
     for j in range(z.half):
         for a in range(z.asks):
-            hit = request == (me ^ j) * z.asks + a
+            hit = request == (me ^ z.offsets[j]) * z.asks + a
             at = z.ask_at + a * z.heads
             ask = jnp.where(hit, near[j][at : at + z.heads, :], ask)
             if a == 0:
                 new = jnp.where(
-                    (request >= 0) & (lax.div(request, z.asks) == (me ^ j)),
+                    (request >= 0) & (lax.div(request, z.asks) == (me ^ z.offsets[j])),
                     near[j][z.new_at : z.pack, :],
                     new,
                 )
@@ -381,7 +383,7 @@
         me = lax.axis_index("seq")
         back[z.pick_at : z.back, :] = asked[...]
         mixed = partial_attention(
-            z, me, me ^ z.half, query, near, table, score_ref, weight_ref, top_ref, sum_ref
+            z, me, me ^ z.far, query, near, table, score_ref, weight_ref, top_ref, sum_ref
         )
         total = sum_ref[...]
         back[0 : z.rows, :] = (mixed / total).astype(jnp.bfloat16)
@@ -458,7 +460,7 @@
     asks, news, scores = [], [], []
     for s in range(z.slots):
         source = lax.div(jnp.maximum(table[s], 0), z.asks)
-        from_far = (source ^ me) >= z.half
+        from_far = ((source ^ me) & z.far) != 0
         here = s * z.heads
         there = z.pick_at + here
         ask = back[there : there + z.heads, :]
@@ -545,7 +547,7 @@
         return pltpu.with_memory_space_constraint(x, pltpu.SMEM)
 
     queries = flat(span_queries)
-    far_queries = local(swap(queries, z.n, z.half))
+    far_queries = local(swap(queries, z.n, z.far))
     packed = pl.pallas_call(
         pack_kernel(z),
         out_shape=pltpu.VMEM((z.pack, z.dim), jnp.bfloat16),
@@ -566,7 +568,7 @@
         flat(decode_new_values),
     )
     near = [local(packed)]
-    for j in range(1, z.half):
+    for j in z.offsets[1:]:
         near.append(local(swap(packed, z.n, j)))
     table = pl.pallas_call(
         plan_kernel(z),
@@ -593,7 +595,7 @@
         scratch_shapes=wide,
         name="far_part",
     )(table, far_queries, local(asked), *near)
-    back = local(swap(sent, z.n, z.half))
+    back = local(swap(sent, z.n, z.far))
     held = pl.pallas_call(
         own_kernel(z),
         out_shape=[

time: 22.3 us -> 22.3 us (level)
  no operation moved by 1% of the time
where the time goes in v2:
time: 22.3 us; the launch traced here: 22.1 us
  starting transfers between devices  10.1 us (45%)
  waiting for transfers between devices  6.94 us (31%)
  Pallas kernels  4.36 us (20%)
  between operations  0.72 us (3%)
    ppermute x5, starting transfers between devices, swap(): return lax.ppermute(x, 'seq', [(i, i ^ by) for i in range(n)])  10.1 us
    ppermute x5, waiting for transfers between devices, swap(): return lax.ppermute(x, 'seq', [(i, i ^ by) for i in range(n)])  6.94 us
    pallas_call x1, Pallas kernels, on_small(): pl.pallas_call(last_kernel(z), out_shape=[jax.ShapeDtypeStruct((z.rows, z...  1.19 us
    pallas_call x1, Pallas kernels, on_small(): pl.pallas_call(pack_kernel(z), out_shape=pltpu.VMEM((z.pack, z.dim), jnp....  0.96 us
    pallas_call x1, Pallas kernels, on_small(): pl.pallas_call(plan_kernel(z), out_shape=pltpu.SMEM((3 * z.slots + z.n,),...  0.93 us
    pallas_call x1, Pallas kernels, on_small(): pl.pallas_call(own_kernel(z), out_shape=[pltpu.VMEM((z.rows, z.dim), jnp....  0.61 us
    pallas_call x1, Pallas kernels, on_small(): pl.pallas_call(far_kernel(z), out_shape=pltpu.VMEM((z.back, z.dim), jnp.b...  0.6 us
  transfers between devices with their start and end apart: 5, of which 2 were waited for; matrix products, arithmetic and copies ran while one was open for 0% of the time, Pallas kernels for 7%

profile of v2, /device:TPU:0, one launch (start us, length us, event | category | flops | bytes accessed | tf_op | source)
XLA Modules:
  0.0 22.1 jit_solution(16118543424621759896)
XLA Ops:
  0.6 0.0 copy-start.2
  0.6 1.0 %pack.1.refs_0_ = bf16[392,128]{1,0:T(8,128)(2,1)S(1)} custom-call(bf16[144,128]{1,0:T(8,128)(2,1)} %bitcast.17, bf16[16,128]{1,0:T(8,128)(2,1)} %bitcast.20, bf16[144,128]{1,0:T(8,128)(2,1)} %bitcast.18, bf16[16,128]{1,0:T(8,128)(2,1)} %bitcast.21, bf16[64,128]{1,0:T(8,128)(2,1)} %bitcast.19, bf16[4,128]{1,0:T(4,128)(2,1)} %bitcast.22, bf16[4,128]{1,0:T(4,128)(2,1)} %bitcast.23), custom_call_target="tpu_custom_call" | custom-call | tf_op jit(solution)/shard_map/pack/pallas_call | solution.py:551
  1.6 4.0 %collective-permute-start.2 = (bf16[392,128]{1,0:T(8,128)(2,1)S(1)}, bf16[392,128]{1,0:T(8,128)(2,1)S(1)}, u32[]{:S(2)}, u32[]{:S(2)}) collective-permute-start(bf16[392,128]{1,0:T(8,128)(2,1)S(1)} %pack.1.refs_0_), channel_id=1, source_target_pairs={{0,6},{2,4},{4,2},{6,0},{8,14},{10,12},{12,10},{14,8},{1,7},{3,5},... | collective-permute-start | bytes 301064 | tf_op jit(solution)/shard_map/ppermute | solution.py:517
  5.7 0.4 %collective-permute-start.1 = (bf16[392,128]{1,0:T(8,128)(2,1)S(1)}, bf16[392,128]{1,0:T(8,128)(2,1)S(1)}, u32[]{:S(2)}, u32[]{:S(2)}) collective-permute-start(bf16[392,128]{1,0:T(8,128)(2,1)S(1)} %pack.1.refs_0_), channel_id=1, source_target_pairs={{0,4},{2,6},{4,0},{6,2},{8,12},{10,14},{12,8},{14,10},{1,5},{3,7},... | collective-permute-start | bytes 301064 | tf_op jit(solution)/shard_map/ppermute | solution.py:517
  6.1 0.2 collective-permute-start
  6.3 0.0 copy-done.2
  6.3 2.9 %collective-permute-start.3 = (bf16[256,128]{1,0:T(8,128)(2,1)S(1)}, bf16[256,128]{1,0:T(8,128)(2,1)S(1)}, u32[]{:S(2)}, u32[]{:S(2)}) collective-permute-start(bf16[256,128]{1,0:T(8,128)(2,1)S(1)} %bitcast.15), channel_id=1, source_target_pairs={{0,8},{2,10},{4,12},{6,14},{8,0},{10,2},{12,4},{14,6},{1,9},{3,11}... | collective-permute-start | bytes 196616 | tf_op jit(solution)/shard_map/ppermute | solution.py:517
  9.2 0.9 %plan.1.table = s32[20]{0:T(128)S(4)} custom-call(s32[16]{0:T(128)} %bitcast.24, s32[8]{0:T(128)} %lengths.1, s32[16]{0:T(128)} %cached.1), custom_call_target="tpu_custom_call" | custom-call | tf_op jit(solution)/shard_map/plan/pallas_call | solution.py:573
  10.2 0.0 collective-permute-done.2.refs_3_
  10.2 2.1 %collective-permute-done.1.refs_2_ = bf16[392,128]{1,0:T(8,128)(2,1)S(1)} collective-permute-done((bf16[392,128]{1,0:T(8,128)(2,1)S(1)}, bf16[392,128]{1,0:T(8,128)(2,1)S(1)}, u32[]{:S(2)}, u32[]{:S(2)}) %collective-permute-start.1) | collective-permute-done | bytes 100384 | tf_op jit(solution)/shard_map/ppermute | solution.py:517
  12.3 0.0 collective-permute-done.refs_1_
  12.3 0.1 select.1.asked
  12.3 0.0 copy-start
  12.4 0.0 copy-start.1
  12.4 0.0 collective-permute-done.3.query
  12.4 0.6 %far_part.1 = bf16[432,128]{1,0:T(8,128)(2,1)S(1)} custom-call(s32[20]{0:T(128)S(4)} %plan.1.table, bf16[256,128]{1,0:T(8,128)(2,1)S(1)} %collective-permute-done.3.query, bf16[160,128]{1,0:T(8,128)(2,1)S(1)} %select.1.asked, bf16[392,128]{1,0:T(8,128)(2,1)S(1)} %pack.1.refs_0_, bf16[392,128]{1,0:T(8,128)(2,1)S(1)} %collective-permute-done.refs_1_, ...), custom_call_target="tpu_custom_call" | custom-call | tf_op jit(solution)/shard_map/far_part/pallas_call | solution.py:590
  13.0 2.5 %collective-permute-start.4 = (bf16[432,128]{1,0:T(8,128)(2,1)S(1)}, bf16[432,128]{1,0:T(8,128)(2,1)S(1)}, u32[]{:S(2)}, u32[]{:S(2)}) collective-permute-start(bf16[432,128]{1,0:T(8,128)(2,1)S(1)} %far_part.1), channel_id=1, source_target_pairs={{0,8},{2,10},{4,12},{6,14},{8,0},{10,2},{12,4},{14,6},{1,9},{3,11}... | collective-permute-start | bytes 331784 | tf_op jit(solution)/shard_map/ppermute | solution.py:517
  15.5 0.6 %own_part.1 = (f32[256,128]{1,0:T(8,128)S(1)}, f32[8,256]{1,0:T(8,128)S(1)}, bf16[160,128]{1,0:T(8,128)(2,1)S(1)}) custom-call(s32[20]{0:T(128)S(4)} %plan.1.table, bf16[256,128]{1,0:T(8,128)(2,1)S(1)} %bitcast.16, bf16[392,128]{1,0:T(8,128)(2,1)S(1)} %pack.1.refs_0_, bf16[392,128]{1,0:T(8,128)(2,1)S(1)} %collective-permute-done.refs_1_, ...), custom_call_target="tpu_custom_call" | custom-call | tf_op jit(solution)/shard_map/own_part/pallas_call | solution.py:599
  16.1 4.8 %collective-permute-done.4.back = bf16[432,128]{1,0:T(8,128)(2,1)S(1)} collective-permute-done((bf16[432,128]{1,0:T(8,128)(2,1)S(1)}, bf16[432,128]{1,0:T(8,128)(2,1)S(1)}, u32[]{:S(2)}, u32[]{:S(2)}) %collective-permute-start.4) | collective-permute-done | bytes 110624 | tf_op jit(solution)/shard_map/ppermute | solution.py:517
  20.9 0.0 copy-done
  20.9 0.0 copy-done.1
  20.9 1.2 %last_part.1 = (bf16[256,128]{1,0:T(8,128)(2,1)}, bf16[128,128]{1,0:T(8,128)(2,1)}) custom-call(s32[20]{0:T(128)S(4)} %plan.1.table, f32[256,128]{1,0:T(8,128)S(1)} %get-tuple-element.7.mixed, f32[8,256]{1,0:T(8,128)S(1)} %get-tuple-element.8.stats, bf16[160,128]{1,0:T(8,128)(2,1)S(1)} %get-tuple-element.9.mine, ...), custom_call_target="tpu_custom_call" | custom-call | tf_op jit(solution)/shard_map/last_part/pallas_call | solution.py:611
Async XLA Ops:
  0.6 5.7 %copy-start.2 = (bf16[8,32,128]{2,1,0:T(8,128)(2,1)S(1)}, bf16[8,32,128]{2,1,0:T(8,128)(2,1)}, u32[]{:S(2)}) copy-start(bf16[8,32,128]{2,1,0:T(8,128)(2,1)} %param.13) | copy-start | bytes 196612
  1.6 8.6 %collective-permute-start.2 = (bf16[392,128]{1,0:T(8,128)(2,1)S(1)}, bf16[392,128]{1,0:T(8,128)(2,1)S(1)}, u32[]{:S(2)}, u32[]{:S(2)}) collective-permute-start(bf16[392,128]{1,0:T(8,128)(2,1)S(1)} %pack.1.refs_0_), channel_id=1, source_target_pairs={{0,6},{2,4},{4,2},{6,0},{8,14},{10,12},{12,10},{14,8},{1,7},{3,5},... | collective-permute-start | bytes 301064 | tf_op jit(solution)/shard_map/ppermute | solution.py:517
  5.7 6.6 %collective-permute-start.1 = (bf16[392,128]{1,0:T(8,128)(2,1)S(1)}, bf16[392,128]{1,0:T(8,128)(2,1)S(1)}, u32[]{:S(2)}, u32[]{:S(2)}) collective-permute-start(bf16[392,128]{1,0:T(8,128)(2,1)S(1)} %pack.1.refs_0_), channel_id=1, source_target_pairs={{0,4},{2,6},{4,0},{6,2},{8,12},{10,14},{12,8},{14,10},{1,5},{3,7},... | collective-permute-start | bytes 301064 | tf_op jit(solution)/shard_map/ppermute | solution.py:517
  6.1 6.2 %collective-permute-start = (bf16[392,128]{1,0:T(8,128)(2,1)S(1)}, bf16[392,128]{1,0:T(8,128)(2,1)S(1)}, u32[]{:S(2)}, u32[]{:S(2)}) collective-permute-start(bf16[392,128]{1,0:T(8,128)(2,1)S(1)} %pack.1.refs_0_), channel_id=1, source_target_pairs={{0,2},{2,0},{4,6},{6,4},{8,10},{10,8},{12,14},{14,12},{1,3},{3,1},... | collective-permute-start | bytes 301064 | tf_op jit(solution)/shard_map/ppermute | solution.py:517
  6.3 6.1 %collective-permute-start.3 = (bf16[256,128]{1,0:T(8,128)(2,1)S(1)}, bf16[256,128]{1,0:T(8,128)(2,1)S(1)}, u32[]{:S(2)}, u32[]{:S(2)}) collective-permute-start(bf16[256,128]{1,0:T(8,128)(2,1)S(1)} %bitcast.15), channel_id=1, source_target_pairs={{0,8},{2,10},{4,12},{6,14},{8,0},{10,2},{12,4},{14,6},{1,9},{3,11}... | collective-permute-start | bytes 196616 | tf_op jit(solution)/shard_map/ppermute | solution.py:517
  12.3 8.6 %copy-start = (bf16[4,256,2,128]{3,2,1,0:T(2,128)(2,1)S(1)}, bf16[4,256,2,128]{3,2,1,0:T(2,128)(2,1)}, u32[]{:S(2)}) copy-start(bf16[4,256,2,128]{3,2,1,0:T(2,128)(2,1)} %param.22) | copy-start | bytes 1572868
  12.4 8.6 %copy-start.1 = (bf16[4,256,2,128]{3,2,1,0:T(2,128)(2,1)S(1)}, bf16[4,256,2,128]{3,2,1,0:T(2,128)(2,1)}, u32[]{:S(2)}) copy-start(bf16[4,256,2,128]{3,2,1,0:T(2,128)(2,1)} %param.23) | copy-start | bytes 1572868
  13.0 7.9 %collective-permute-start.4 = (bf16[432,128]{1,0:T(8,128)(2,1)S(1)}, bf16[432,128]{1,0:T(8,128)(2,1)S(1)}, u32[]{:S(2)}, u32[]{:S(2)}) collective-permute-start(bf16[432,128]{1,0:T(8,128)(2,1)S(1)} %far_part.1), channel_id=1, source_target_pairs={{0,8},{2,10},{4,12},{6,14},{8,0},{10,2},{12,4},{14,6},{1,9},{3,11}... | collective-permute-start | bytes 331784 | tf_op jit(solution)/shard_map/ppermute | solution.py:517

commit v3 on v2

--- a/solution.py
+++ b/solution.py
@@ -219,7 +219,7 @@
         self.stat_rows = PIECES * self.rows // self.dim
         self.pick_at = self.rows + self.stat_rows
         self.pick_new_at = self.slots * self.heads
-        self.picks = self.pick_new_at + self.slots * self.new_rows
+        self.picks = self.pick_new_at + self.slots // 2 * self.new_rows
         self.back = self.pick_at + self.picks
         self.factor = self.dim**-0.5 * math.log2(math.e)
 
@@ -234,7 +234,9 @@
             and self.block % 16 == 0
             and self.cols % 128 == 0
             and self.cache_rows % 128 == 0
-            and self.new_rows == 8
+            and self.kv == 2
+            and self.asks == 2
+            and self.slots % 4 == 0
         )
 
 
@@ -362,11 +364,19 @@
 
 
 def pick_all(z, me, table, first, near, out):
+    upper = (lax.broadcasted_iota(jnp.int32, (z.new_rows, z.dim), 0) & 2) == 0
+    tiles = []
     for s in range(z.slots):
-        ask, new = pick_near(z, me, near, table[first + s])
+        request = table[first + s]
+        ask, new = pick_near(z, me, near, request)
         out[s * z.heads : (s + 1) * z.heads, :] = ask
-        at = z.pick_new_at + s * z.new_rows
-        out[at : at + z.new_rows, :] = new
+        new = new.astype(jnp.float32)
+        crossed = jnp.where(upper, pltpu.roll(new, z.new_rows - 2, 0), pltpu.roll(new, 2, 0))
+        tiles.append(jnp.where((request & 1) == s % 2, new, crossed))
+    for p in range(z.slots // 2):
+        at = z.pick_new_at + p * z.new_rows
+        tile = jnp.where(upper, tiles[2 * p], tiles[2 * p + 1])
+        out[at : at + z.new_rows, :] = tile.astype(jnp.bfloat16)
 
 
 def select_kernel(z):
@@ -465,7 +475,7 @@
         there = z.pick_at + here
         ask = back[there : there + z.heads, :]
         asks.append(jnp.where(from_far, ask, mine[here : here + z.heads, :]))
-        here = z.pick_new_at + s * z.new_rows
+        here = z.pick_new_at + s // 2 * z.new_rows
         there = z.pick_at + here
         new = back[there : there + z.new_rows, :]
         new = jnp.where(from_far, new, mine[here : here + z.new_rows, :])
@@ -481,18 +491,11 @@
         )
     weights, rests = [], []
     for s in range(z.slots):
-        safe = jnp.maximum(table[s], 0)
-        at = safe - lax.div(safe, z.asks) * z.asks
         new = news[s]
-        new_key = jnp.zeros((z.heads, z.dim), jnp.float32)
-        new_value = jnp.zeros((z.heads, z.dim), jnp.float32)
-        for a in range(z.asks):
-            for h in range(z.kv):
-                here_now = (head_of == h) & (at == a)
-                i = a * z.kv + h
-                new_key = jnp.where(here_now, new[i : i + 1, :], new_key)
-                i = i + z.asks * z.kv
-                new_value = jnp.where(here_now, new[i : i + 1, :], new_value)
+        i = s % 2 * z.kv
+        new_key = jnp.where(head_of == 0, new[i : i + 1, :], new[i + 1 : i + 2, :])
+        i = i + z.asks * z.kv
+        new_value = jnp.where(head_of == 0, new[i : i + 1, :], new[i + 1 : i + 2, :])
         own = jnp.sum(asks[s].astype(jnp.float32) * new_key, axis=-1, keepdims=True)
         seen = jnp.where(match & (place < table[2 * z.slots + s]), scores[s], LOWEST)
         peak = jnp.maximum(jnp.max(seen, axis=-1, keepdims=True), own)

time: 22.3 us -> 22.2 us (level)
  no operation moved by 1% of the time
where the time goes in v3:
time: 22.2 us; the launch traced here: 22 us
  starting transfers between devices  10.1 us (45%)
  waiting for transfers between devices  6.81 us (31%)
  Pallas kernels  4.35 us (20%)
  between operations  0.71 us (3%)
    ppermute x5, starting transfers between devices, swap(): return lax.ppermute(x, 'seq', [(i, i ^ by) for i in range(n)])  10.1 us
    ppermute x5, waiting for transfers between devices, swap(): return lax.ppermute(x, 'seq', [(i, i ^ by) for i in range(n)])  6.81 us
    pallas_call x1, Pallas kernels, on_small(): pl.pallas_call(last_kernel(z), out_shape=[jax.ShapeDtypeStruct((z.rows, z...  1.18 us
    pallas_call x1, Pallas kernels, on_small(): pl.pallas_call(pack_kernel(z), out_shape=pltpu.VMEM((z.pack, z.dim), jnp....  0.96 us
    pallas_call x1, Pallas kernels, on_small(): pl.pallas_call(plan_kernel(z), out_shape=pltpu.SMEM((3 * z.slots + z.n,),...  0.93 us
    pallas_call x1, Pallas kernels, on_small(): pl.pallas_call(own_kernel(z), out_shape=[pltpu.VMEM((z.rows, z.dim), jnp....  0.61 us
    pallas_call x1, Pallas kernels, on_small(): pl.pallas_call(far_kernel(z), out_shape=pltpu.VMEM((z.back, z.dim), jnp.b...  0.6 us
  transfers between devices with their start and end apart: 5, of which 2 were waited for; matrix products, arithmetic and copies ran while one was open for 0% of the time, Pallas kernels for 7%

profile of v3, /device:TPU:0, one launch (start us, length us, event | category | flops | bytes accessed | tf_op | source)
XLA Modules:
  0.0 22.0 jit_solution(3608357692635084401)
XLA Ops:
  0.6 0.0 copy-start.2
  0.6 1.0 %pack.1.refs_0_ = bf16[392,128]{1,0:T(8,128)(2,1)S(1)} custom-call(bf16[144,128]{1,0:T(8,128)(2,1)} %bitcast.17, bf16[16,128]{1,0:T(8,128)(2,1)} %bitcast.20, bf16[144,128]{1,0:T(8,128)(2,1)} %bitcast.18, bf16[16,128]{1,0:T(8,128)(2,1)} %bitcast.21, bf16[64,128]{1,0:T(8,128)(2,1)} %bitcast.19, bf16[4,128]{1,0:T(4,128)(2,1)} %bitcast.22, bf16[4,128]{1,0:T(4,128)(2,1)} %bitcast.23), custom_call_target="tpu_custom_call" | custom-call | tf_op jit(solution)/shard_map/pack/pallas_call | solution.py:554
  1.6 4.0 %collective-permute-start.2 = (bf16[392,128]{1,0:T(8,128)(2,1)S(1)}, bf16[392,128]{1,0:T(8,128)(2,1)S(1)}, u32[]{:S(2)}, u32[]{:S(2)}) collective-permute-start(bf16[392,128]{1,0:T(8,128)(2,1)S(1)} %pack.1.refs_0_), channel_id=1, source_target_pairs={{0,6},{2,4},{4,2},{6,0},{8,14},{10,12},{12,10},{14,8},{1,7},{3,5},... | collective-permute-start | bytes 301064 | tf_op jit(solution)/shard_map/ppermute | solution.py:520
  5.7 0.4 %collective-permute-start.1 = (bf16[392,128]{1,0:T(8,128)(2,1)S(1)}, bf16[392,128]{1,0:T(8,128)(2,1)S(1)}, u32[]{:S(2)}, u32[]{:S(2)}) collective-permute-start(bf16[392,128]{1,0:T(8,128)(2,1)S(1)} %pack.1.refs_0_), channel_id=1, source_target_pairs={{0,4},{2,6},{4,0},{6,2},{8,12},{10,14},{12,8},{14,10},{1,5},{3,7},... | collective-permute-start | bytes 301064 | tf_op jit(solution)/shard_map/ppermute | solution.py:520
  6.1 0.2 collective-permute-start
  6.3 0.0 copy-done.2
  6.3 2.9 %collective-permute-start.3 = (bf16[256,128]{1,0:T(8,128)(2,1)S(1)}, bf16[256,128]{1,0:T(8,128)(2,1)S(1)}, u32[]{:S(2)}, u32[]{:S(2)}) collective-permute-start(bf16[256,128]{1,0:T(8,128)(2,1)S(1)} %bitcast.15), channel_id=1, source_target_pairs={{0,8},{2,10},{4,12},{6,14},{8,0},{10,2},{12,4},{14,6},{1,9},{3,11}... | collective-permute-start | bytes 196616 | tf_op jit(solution)/shard_map/ppermute | solution.py:520
  9.2 0.9 %plan.1.table = s32[20]{0:T(128)S(4)} custom-call(s32[16]{0:T(128)} %bitcast.24, s32[8]{0:T(128)} %lengths.1, s32[16]{0:T(128)} %cached.1), custom_call_target="tpu_custom_call" | custom-call | tf_op jit(solution)/shard_map/plan/pallas_call | solution.py:576
  10.2 0.0 collective-permute-done.2.refs_3_
  10.2 2.1 %collective-permute-done.1.refs_2_ = bf16[392,128]{1,0:T(8,128)(2,1)S(1)} collective-permute-done((bf16[392,128]{1,0:T(8,128)(2,1)S(1)}, bf16[392,128]{1,0:T(8,128)(2,1)S(1)}, u32[]{:S(2)}, u32[]{:S(2)}) %collective-permute-start.1) | collective-permute-done | bytes 100384 | tf_op jit(solution)/shard_map/ppermute | solution.py:520
  12.3 0.0 collective-permute-done.refs_1_
  12.3 0.1 select.1.asked
  12.4 0.0 copy-start
  12.4 0.0 copy-start.1
  12.4 0.0 collective-permute-done.3.query
  12.4 0.6 %far_part.1 = bf16[416,128]{1,0:T(8,128)(2,1)S(1)} custom-call(s32[20]{0:T(128)S(4)} %plan.1.table, bf16[256,128]{1,0:T(8,128)(2,1)S(1)} %collective-permute-done.3.query, bf16[144,128]{1,0:T(8,128)(2,1)S(1)} %select.1.asked, bf16[392,128]{1,0:T(8,128)(2,1)S(1)} %pack.1.refs_0_, bf16[392,128]{1,0:T(8,128)(2,1)S(1)} %collective-permute-done.refs_1_, ...), custom_call_target="tpu_custom_call" | custom-call | tf_op jit(solution)/shard_map/far_part/pallas_call | solution.py:593
  13.0 2.5 %collective-permute-start.4 = (bf16[416,128]{1,0:T(8,128)(2,1)S(1)}, bf16[416,128]{1,0:T(8,128)(2,1)S(1)}, u32[]{:S(2)}, u32[]{:S(2)}) collective-permute-start(bf16[416,128]{1,0:T(8,128)(2,1)S(1)} %far_part.1), channel_id=1, source_target_pairs={{0,8},{2,10},{4,12},{6,14},{8,0},{10,2},{12,4},{14,6},{1,9},{3,11}... | collective-permute-start | bytes 319496 | tf_op jit(solution)/shard_map/ppermute | solution.py:520
  15.5 0.6 %own_part.1 = (f32[256,128]{1,0:T(8,128)S(1)}, f32[8,256]{1,0:T(8,128)S(1)}, bf16[144,128]{1,0:T(8,128)(2,1)S(1)}) custom-call(s32[20]{0:T(128)S(4)} %plan.1.table, bf16[256,128]{1,0:T(8,128)(2,1)S(1)} %bitcast.16, bf16[392,128]{1,0:T(8,128)(2,1)S(1)} %pack.1.refs_0_, bf16[392,128]{1,0:T(8,128)(2,1)S(1)} %collective-permute-done.refs_1_, ...), custom_call_target="tpu_custom_call" | custom-call | tf_op jit(solution)/shard_map/own_part/pallas_call | solution.py:602
  16.1 4.7 %collective-permute-done.4.back = bf16[416,128]{1,0:T(8,128)(2,1)S(1)} collective-permute-done((bf16[416,128]{1,0:T(8,128)(2,1)S(1)}, bf16[416,128]{1,0:T(8,128)(2,1)S(1)}, u32[]{:S(2)}, u32[]{:S(2)}) %collective-permute-start.4) | collective-permute-done | bytes 106528 | tf_op jit(solution)/shard_map/ppermute | solution.py:520
  20.8 0.0 copy-done
  20.8 0.0 copy-done.1
  20.8 1.2 %last_part.1 = (bf16[256,128]{1,0:T(8,128)(2,1)}, bf16[128,128]{1,0:T(8,128)(2,1)}) custom-call(s32[20]{0:T(128)S(4)} %plan.1.table, f32[256,128]{1,0:T(8,128)S(1)} %get-tuple-element.7.mixed, f32[8,256]{1,0:T(8,128)S(1)} %get-tuple-element.8.stats, bf16[144,128]{1,0:T(8,128)(2,1)S(1)} %get-tuple-element.9.mine, ...), custom_call_target="tpu_custom_call" | custom-call | tf_op jit(solution)/shard_map/last_part/pallas_call | solution.py:614
Async XLA Ops:
  0.6 5.7 %copy-start.2 = (bf16[8,32,128]{2,1,0:T(8,128)(2,1)S(1)}, bf16[8,32,128]{2,1,0:T(8,128)(2,1)}, u32[]{:S(2)}) copy-start(bf16[8,32,128]{2,1,0:T(8,128)(2,1)} %param.13) | copy-start | bytes 196612
  1.6 8.6 %collective-permute-start.2 = (bf16[392,128]{1,0:T(8,128)(2,1)S(1)}, bf16[392,128]{1,0:T(8,128)(2,1)S(1)}, u32[]{:S(2)}, u32[]{:S(2)}) collective-permute-start(bf16[392,128]{1,0:T(8,128)(2,1)S(1)} %pack.1.refs_0_), channel_id=1, source_target_pairs={{0,6},{2,4},{4,2},{6,0},{8,14},{10,12},{12,10},{14,8},{1,7},{3,5},... | collective-permute-start | bytes 301064 | tf_op jit(solution)/shard_map/ppermute | solution.py:520
  5.7 6.6 %collective-permute-start.1 = (bf16[392,128]{1,0:T(8,128)(2,1)S(1)}, bf16[392,128]{1,0:T(8,128)(2,1)S(1)}, u32[]{:S(2)}, u32[]{:S(2)}) collective-permute-start(bf16[392,128]{1,0:T(8,128)(2,1)S(1)} %pack.1.refs_0_), channel_id=1, source_target_pairs={{0,4},{2,6},{4,0},{6,2},{8,12},{10,14},{12,8},{14,10},{1,5},{3,7},... | collective-permute-start | bytes 301064 | tf_op jit(solution)/shard_map/ppermute | solution.py:520
  6.1 6.2 %collective-permute-start = (bf16[392,128]{1,0:T(8,128)(2,1)S(1)}, bf16[392,128]{1,0:T(8,128)(2,1)S(1)}, u32[]{:S(2)}, u32[]{:S(2)}) collective-permute-start(bf16[392,128]{1,0:T(8,128)(2,1)S(1)} %pack.1.refs_0_), channel_id=1, source_target_pairs={{0,2},{2,0},{4,6},{6,4},{8,10},{10,8},{12,14},{14,12},{1,3},{3,1},... | collective-permute-start | bytes 301064 | tf_op jit(solution)/shard_map/ppermute | solution.py:520
  6.3 6.1 %collective-permute-start.3 = (bf16[256,128]{1,0:T(8,128)(2,1)S(1)}, bf16[256,128]{1,0:T(8,128)(2,1)S(1)}, u32[]{:S(2)}, u32[]{:S(2)}) collective-permute-start(bf16[256,128]{1,0:T(8,128)(2,1)S(1)} %bitcast.15), channel_id=1, source_target_pairs={{0,8},{2,10},{4,12},{6,14},{8,0},{10,2},{12,4},{14,6},{1,9},{3,11}... | collective-permute-start | bytes 196616 | tf_op jit(solution)/shard_map/ppermute | solution.py:520
  12.4 8.4 %copy-start = (bf16[4,256,2,128]{3,2,1,0:T(2,128)(2,1)S(1)}, bf16[4,256,2,128]{3,2,1,0:T(2,128)(2,1)}, u32[]{:S(2)}) copy-start(bf16[4,256,2,128]{3,2,1,0:T(2,128)(2,1)} %param.22) | copy-start | bytes 1572868
  12.4 8.4 %copy-start.1 = (bf16[4,256,2,128]{3,2,1,0:T(2,128)(2,1)S(1)}, bf16[4,256,2,128]{3,2,1,0:T(2,128)(2,1)}, u32[]{:S(2)}) copy-start(bf16[4,256,2,128]{3,2,1,0:T(2,128)(2,1)} %param.23) | copy-start | bytes 1572868
  13.0 7.8 %collective-permute-start.4 = (bf16[416,128]{1,0:T(8,128)(2,1)S(1)}, bf16[416,128]{1,0:T(8,128)(2,1)S(1)}, u32[]{:S(2)}, u32[]{:S(2)}) collective-permute-start(bf16[416,128]{1,0:T(8,128)(2,1)S(1)} %far_part.1), channel_id=1, source_target_pairs={{0,8},{2,10},{4,12},{6,14},{8,0},{10,2},{12,4},{14,6},{1,9},{3,11}... | collective-permute-start | bytes 319496 | tf_op jit(solution)/shard_map/ppermute | solution.py:520

commit v4 on v3

--- a/solution.py
+++ b/solution.py
@@ -348,12 +348,14 @@
             into = out.at[pl.ds(at, rows), :] if i < 5 else new.at[i - 5]
             copies.append(pltpu.make_async_copy(ref, into, sems.at[i]))
             at += rows
-        for copy in reversed(copies):
+        for copy in copies:
             copy.start()
-        for copy in reversed(copies):
+        for copy in copies[5:]:
             copy.wait()
         both = [new[i].astype(jnp.float32) for i in range(2)]
         out[z.new_at : z.pack, :] = jnp.concatenate(both, axis=0).astype(jnp.bfloat16)
+        for copy in copies[:5]:
+            copy.wait()
 
     return body
 

time: 22.2 us -> 22.1 us (level)
  no operation moved by 1% of the time
where the time goes in v4:
time: 22.1 us; the launch traced here: 21.9 us
  starting transfers between devices  10.1 us (46%)
  waiting for transfers between devices  6.81 us (31%)
  Pallas kernels  4.29 us (19%)
  between operations  0.71 us (3%)
    ppermute x5, starting transfers between devices, swap(): return lax.ppermute(x, 'seq', [(i, i ^ by) for i in range(n)])  10.1 us
    ppermute x5, waiting for transfers between devices, swap(): return lax.ppermute(x, 'seq', [(i, i ^ by) for i in range(n)])  6.81 us
    pallas_call x1, Pallas kernels, on_small(): pl.pallas_call(last_kernel(z), out_shape=[jax.ShapeDtypeStruct((z.rows, z...  1.18 us
    pallas_call x1, Pallas kernels, on_small(): pl.pallas_call(plan_kernel(z), out_shape=pltpu.SMEM((3 * z.slots + z.n,),...  0.93 us
    pallas_call x1, Pallas kernels, on_small(): pl.pallas_call(pack_kernel(z), out_shape=pltpu.VMEM((z.pack, z.dim), jnp....  0.9 us
    pallas_call x1, Pallas kernels, on_small(): pl.pallas_call(own_kernel(z), out_shape=[pltpu.VMEM((z.rows, z.dim), jnp....  0.6 us
    pallas_call x1, Pallas kernels, on_small(): pl.pallas_call(far_kernel(z), out_shape=pltpu.VMEM((z.back, z.dim), jnp.b...  0.6 us
  transfers between devices with their start and end apart: 5, of which 2 were waited for; matrix products, arithmetic and copies ran while one was open for 0% of the time, Pallas kernels for 7%

profile of v4, /device:TPU:0, one launch (start us, length us, event | category | flops | bytes accessed | tf_op | source)
XLA Modules:
  0.0 21.9 jit_solution(7663073125394602852)
XLA Ops:
  0.6 0.0 copy-start.2
  0.6 0.9 %pack.1.refs_0_ = bf16[392,128]{1,0:T(8,128)(2,1)S(1)} custom-call(bf16[144,128]{1,0:T(8,128)(2,1)} %bitcast.17, bf16[16,128]{1,0:T(8,128)(2,1)} %bitcast.20, bf16[144,128]{1,0:T(8,128)(2,1)} %bitcast.18, bf16[16,128]{1,0:T(8,128)(2,1)} %bitcast.21, bf16[64,128]{1,0:T(8,128)(2,1)} %bitcast.19, bf16[4,128]{1,0:T(4,128)(2,1)} %bitcast.22, bf16[4,128]{1,0:T(4,128)(2,1)} %bitcast.23), custom_call_target="tpu_custom_call" | custom-call | tf_op jit(solution)/shard_map/pack/pallas_call | solution.py:556
  1.5 4.0 %collective-permute-start.2 = (bf16[392,128]{1,0:T(8,128)(2,1)S(1)}, bf16[392,128]{1,0:T(8,128)(2,1)S(1)}, u32[]{:S(2)}, u32[]{:S(2)}) collective-permute-start(bf16[392,128]{1,0:T(8,128)(2,1)S(1)} %pack.1.refs_0_), channel_id=1, source_target_pairs={{0,6},{2,4},{4,2},{6,0},{8,14},{10,12},{12,10},{14,8},{1,7},{3,5},... | collective-permute-start | bytes 301064 | tf_op jit(solution)/shard_map/ppermute | solution.py:522
  5.6 0.4 %collective-permute-start.1 = (bf16[392,128]{1,0:T(8,128)(2,1)S(1)}, bf16[392,128]{1,0:T(8,128)(2,1)S(1)}, u32[]{:S(2)}, u32[]{:S(2)}) collective-permute-start(bf16[392,128]{1,0:T(8,128)(2,1)S(1)} %pack.1.refs_0_), channel_id=1, source_target_pairs={{0,4},{2,6},{4,0},{6,2},{8,12},{10,14},{12,8},{14,10},{1,5},{3,7},... | collective-permute-start | bytes 301064 | tf_op jit(solution)/shard_map/ppermute | solution.py:522
  6.0 0.2 collective-permute-start
  6.2 0.0 copy-done.2
  6.2 2.9 %collective-permute-start.3 = (bf16[256,128]{1,0:T(8,128)(2,1)S(1)}, bf16[256,128]{1,0:T(8,128)(2,1)S(1)}, u32[]{:S(2)}, u32[]{:S(2)}) collective-permute-start(bf16[256,128]{1,0:T(8,128)(2,1)S(1)} %bitcast.15), channel_id=1, source_target_pairs={{0,8},{2,10},{4,12},{6,14},{8,0},{10,2},{12,4},{14,6},{1,9},{3,11}... | collective-permute-start | bytes 196616 | tf_op jit(solution)/shard_map/ppermute | solution.py:522
  9.2 0.9 %plan.1.table = s32[20]{0:T(128)S(4)} custom-call(s32[16]{0:T(128)} %bitcast.24, s32[8]{0:T(128)} %lengths.1, s32[16]{0:T(128)} %cached.1), custom_call_target="tpu_custom_call" | custom-call | tf_op jit(solution)/shard_map/plan/pallas_call | solution.py:578
  10.1 0.0 collective-permute-done.2.refs_3_
  10.1 2.1 %collective-permute-done.1.refs_2_ = bf16[392,128]{1,0:T(8,128)(2,1)S(1)} collective-permute-done((bf16[392,128]{1,0:T(8,128)(2,1)S(1)}, bf16[392,128]{1,0:T(8,128)(2,1)S(1)}, u32[]{:S(2)}, u32[]{:S(2)}) %collective-permute-start.1) | collective-permute-done | bytes 100384 | tf_op jit(solution)/shard_map/ppermute | solution.py:522
  12.2 0.0 collective-permute-done.refs_1_
  12.2 0.1 select.1.asked
  12.3 0.0 copy-start
  12.3 0.0 copy-start.1
  12.3 0.0 collective-permute-done.3.query
  12.3 0.6 %far_part.1 = bf16[416,128]{1,0:T(8,128)(2,1)S(1)} custom-call(s32[20]{0:T(128)S(4)} %plan.1.table, bf16[256,128]{1,0:T(8,128)(2,1)S(1)} %collective-permute-done.3.query, bf16[144,128]{1,0:T(8,128)(2,1)S(1)} %select.1.asked, bf16[392,128]{1,0:T(8,128)(2,1)S(1)} %pack.1.refs_0_, bf16[392,128]{1,0:T(8,128)(2,1)S(1)} %collective-permute-done.refs_1_, ...), custom_call_target="tpu_custom_call" | custom-call | tf_op jit(solution)/shard_map/far_part/pallas_call | solution.py:595
  12.9 2.5 %collective-permute-start.4 = (bf16[416,128]{1,0:T(8,128)(2,1)S(1)}, bf16[416,128]{1,0:T(8,128)(2,1)S(1)}, u32[]{:S(2)}, u32[]{:S(2)}) collective-permute-start(bf16[416,128]{1,0:T(8,128)(2,1)S(1)} %far_part.1), channel_id=1, source_target_pairs={{0,8},{2,10},{4,12},{6,14},{8,0},{10,2},{12,4},{14,6},{1,9},{3,11}... | collective-permute-start | bytes 319496 | tf_op jit(solution)/shard_map/ppermute | solution.py:522
  15.4 0.6 %own_part.1 = (f32[256,128]{1,0:T(8,128)S(1)}, f32[8,256]{1,0:T(8,128)S(1)}, bf16[144,128]{1,0:T(8,128)(2,1)S(1)}) custom-call(s32[20]{0:T(128)S(4)} %plan.1.table, bf16[256,128]{1,0:T(8,128)(2,1)S(1)} %bitcast.16, bf16[392,128]{1,0:T(8,128)(2,1)S(1)} %pack.1.refs_0_, bf16[392,128]{1,0:T(8,128)(2,1)S(1)} %collective-permute-done.refs_1_, ...), custom_call_target="tpu_custom_call" | custom-call | tf_op jit(solution)/shard_map/own_part/pallas_call | solution.py:604
  16.0 4.7 %collective-permute-done.4.back = bf16[416,128]{1,0:T(8,128)(2,1)S(1)} collective-permute-done((bf16[416,128]{1,0:T(8,128)(2,1)S(1)}, bf16[416,128]{1,0:T(8,128)(2,1)S(1)}, u32[]{:S(2)}, u32[]{:S(2)}) %collective-permute-start.4) | collective-permute-done | bytes 106528 | tf_op jit(solution)/shard_map/ppermute | solution.py:522
  20.7 0.0 copy-done
  20.7 0.0 copy-done.1
  20.7 1.2 %last_part.1 = (bf16[256,128]{1,0:T(8,128)(2,1)}, bf16[128,128]{1,0:T(8,128)(2,1)}) custom-call(s32[20]{0:T(128)S(4)} %plan.1.table, f32[256,128]{1,0:T(8,128)S(1)} %get-tuple-element.7.mixed, f32[8,256]{1,0:T(8,128)S(1)} %get-tuple-element.8.stats, bf16[144,128]{1,0:T(8,128)(2,1)S(1)} %get-tuple-element.9.mine, ...), custom_call_target="tpu_custom_call" | custom-call | tf_op jit(solution)/shard_map/last_part/pallas_call | solution.py:616
Async XLA Ops:
  0.6 5.6 %copy-start.2 = (bf16[8,32,128]{2,1,0:T(8,128)(2,1)S(1)}, bf16[8,32,128]{2,1,0:T(8,128)(2,1)}, u32[]{:S(2)}) copy-start(bf16[8,32,128]{2,1,0:T(8,128)(2,1)} %param.13) | copy-start | bytes 196612
  1.5 8.6 %collective-permute-start.2 = (bf16[392,128]{1,0:T(8,128)(2,1)S(1)}, bf16[392,128]{1,0:T(8,128)(2,1)S(1)}, u32[]{:S(2)}, u32[]{:S(2)}) collective-permute-start(bf16[392,128]{1,0:T(8,128)(2,1)S(1)} %pack.1.refs_0_), channel_id=1, source_target_pairs={{0,6},{2,4},{4,2},{6,0},{8,14},{10,12},{12,10},{14,8},{1,7},{3,5},... | collective-permute-start | bytes 301064 | tf_op jit(solution)/shard_map/ppermute | solution.py:522
  5.6 6.6 %collective-permute-start.1 = (bf16[392,128]{1,0:T(8,128)(2,1)S(1)}, bf16[392,128]{1,0:T(8,128)(2,1)S(1)}, u32[]{:S(2)}, u32[]{:S(2)}) collective-permute-start(bf16[392,128]{1,0:T(8,128)(2,1)S(1)} %pack.1.refs_0_), channel_id=1, source_target_pairs={{0,4},{2,6},{4,0},{6,2},{8,12},{10,14},{12,8},{14,10},{1,5},{3,7},... | collective-permute-start | bytes 301064 | tf_op jit(solution)/shard_map/ppermute | solution.py:522
  6.0 6.2 %collective-permute-start = (bf16[392,128]{1,0:T(8,128)(2,1)S(1)}, bf16[392,128]{1,0:T(8,128)(2,1)S(1)}, u32[]{:S(2)}, u32[]{:S(2)}) collective-permute-start(bf16[392,128]{1,0:T(8,128)(2,1)S(1)} %pack.1.refs_0_), channel_id=1, source_target_pairs={{0,2},{2,0},{4,6},{6,4},{8,10},{10,8},{12,14},{14,12},{1,3},{3,1},... | collective-permute-start | bytes 301064 | tf_op jit(solution)/shard_map/ppermute | solution.py:522
  6.2 6.1 %collective-permute-start.3 = (bf16[256,128]{1,0:T(8,128)(2,1)S(1)}, bf16[256,128]{1,0:T(8,128)(2,1)S(1)}, u32[]{:S(2)}, u32[]{:S(2)}) collective-permute-start(bf16[256,128]{1,0:T(8,128)(2,1)S(1)} %bitcast.15), channel_id=1, source_target_pairs={{0,8},{2,10},{4,12},{6,14},{8,0},{10,2},{12,4},{14,6},{1,9},{3,11}... | collective-permute-start | bytes 196616 | tf_op jit(solution)/shard_map/ppermute | solution.py:522
  12.3 8.4 %copy-start = (bf16[4,256,2,128]{3,2,1,0:T(2,128)(2,1)S(1)}, bf16[4,256,2,128]{3,2,1,0:T(2,128)(2,1)}, u32[]{:S(2)}) copy-start(bf16[4,256,2,128]{3,2,1,0:T(2,128)(2,1)} %param.22) | copy-start | bytes 1572868
  12.3 8.4 %copy-start.1 = (bf16[4,256,2,128]{3,2,1,0:T(2,128)(2,1)S(1)}, bf16[4,256,2,128]{3,2,1,0:T(2,128)(2,1)}, u32[]{:S(2)}) copy-start(bf16[4,256,2,128]{3,2,1,0:T(2,128)(2,1)} %param.23) | copy-start | bytes 1572868
  12.9 7.8 %collective-permute-start.4 = (bf16[416,128]{1,0:T(8,128)(2,1)S(1)}, bf16[416,128]{1,0:T(8,128)(2,1)S(1)}, u32[]{:S(2)}, u32[]{:S(2)}) collective-permute-start(bf16[416,128]{1,0:T(8,128)(2,1)S(1)} %far_part.1), channel_id=1, source_target_pairs={{0,8},{2,10},{4,12},{6,14},{8,0},{10,2},{12,4},{14,6},{1,9},{3,11}... | collective-permute-start | bytes 319496 | tf_op jit(solution)/shard_map/ppermute | solution.py:522
